TPU v7x, 32 devices: a whole 2x2x4 slice. The times are simulated.
32 devices in a mesh: grp: 4 (over z), kv: 4 (over y, x), tp: 2 (over core).
Axes of the slice: x: 2, y: 2, z: 4, core: 2. Of those that a mesh axis runs over, the one named last changes fastest.
Arguments:
- hidden_states: bfloat16 [512, 4096], P('grp', 'kv'), may hold values from -6 to 6
- attn_gain: float32 [4096], P('kv'), may hold values from 0.25 to 1.75
- mlp_gain: float32 [4096], replicated, may hold values from 0.25 to 1.75
- w_query: bfloat16 [4096, 4096], P('kv', 'tp'), may hold values from -0.09375 to 0.09375
- w_out: bfloat16 [32, 128, 4096], P('tp', 'kv'), may hold values from -1 to 1
- w_gate: bfloat16 [4096, 14336], P(None, ('kv', 'tp')), may hold values from -0.09375 to 0.09375
- w_up: bfloat16 [4096, 14336], P(None, ('kv', 'tp')), may hold values from -0.09375 to 0.09375
- w_down: bfloat16 [14336, 4096], P(('kv', 'tp')), may hold values from -0.046875 to 0.046875
- kv_pool: bfloat16 [256, 2, 128, 1024], P(('grp', 'kv'), None, None, 'tp'), may hold values from -110 to 110
- resident_cache: bfloat16 [4, 32, 2, 128, 1024], P('grp', 'kv', None, None, 'tp'), may hold values from -110 to 110
- resident_slot: int32 [4, 32], P('grp', 'kv'), may hold values from 0 to 127
- resident_len: int32 [4, 32], P('grp', 'kv'), may hold values from 1 to 128
- new_owner: int32 [4, 64], replicated, may hold values from 0 to 15, as said below
- new_local: int32 [4, 64], replicated, may hold values from 0 to 15
- new_slot: int32 [4, 64], P('grp', 'kv'), may hold values from 0 to 127
- new_len: int32 [4, 64], P('grp', 'kv'), may hold values from 1 to 128
- token_kv: bfloat16 [512, 2, 1024], P('grp', None, 'tp'), may hold values from -6 to 6
Outputs:
- mixed: bfloat16 [512, 4096], P(('grp', 'kv', 'tp'))
- new_cache: bfloat16 [4, 64, 2, 128, 1024], P('grp', 'kv', None, None, 'tp')
Inputs may be any that keep to these rules, and one draw needn't show every extreme that they name: New page c of group g is kept by the device of kv index c // 16 of group g and comes from the device whose index along grp+kv is new_owner[g, c]; every decode device receives exactly 4 new pages from the owners of each grp index; no owner sends more than 4 pages to the devices of one kv index over all groups, so at most 4 to one device; every owner sends each of its 16 pages exactly once.
All inputs are finite; a program needn't handle non-finite values.
Results may differ from a plain program's by a relative error of at most 0.018.
Values may be sent and summed in bfloat16 or wider, within the bound.
A program may use at most 128 MiB of HBM per device.

v0:
```python
import functools

import jax
import jax.numpy as jnp
from jax import lax
from jax.experimental import pallas as pl
from jax.experimental.pallas import tpu as pltpu
from jax.sharding import PartitionSpec as P

D = 4096
HEADS = 32
KV_HEADS = 8
HEAD_DIM = 128
NPR = 4


neg_fill = -1e30
norm_eps = 1e-05


def push_kernel(axes, spread, src, out, send_sem, recv_sem, own_sem):
    sizes = [lax.axis_size(axis) for axis in axes]
    count = 1
    me = jnp.int32(0)
    for axis, size in zip(axes, sizes):
        me = me * size + lax.axis_index(axis)
        count *= size

    def device(index):
        where = {}
        for axis, size in reversed(list(zip(axes, sizes))):
            where[axis] = lax.rem(index, size)
            index = index // size
        return where

    barrier = pltpu.get_barrier_semaphore()
    for step in range(1, count):
        pl.semaphore_signal(
            barrier,
            inc=1,
            device_id=device(lax.rem(me + step, count)),
            device_id_type=pl.DeviceIdType.MESH,
        )
    pl.semaphore_wait(barrier, count - 1)
    copies = []
    for step in range(1, count):
        peer = lax.rem(me + step, count)
        copy = pltpu.make_async_remote_copy(
            src_ref=src if spread else src.at[peer],
            dst_ref=out.at[me],
            send_sem=send_sem.at[step],
            recv_sem=recv_sem.at[step],
            device_id=device(peer),
            device_id_type=pl.DeviceIdType.MESH,
        )
        copy.start()
        copies.append(copy)
    own = pltpu.make_async_copy(src if spread else src.at[me], out.at[me], own_sem)
    own.start()
    own.wait()
    for step in range(1, count):
        source = lax.rem(me - step + count, count)
        pltpu.make_async_remote_copy(
            src_ref=src if spread else src.at[source],
            dst_ref=out.at[source],
            send_sem=send_sem.at[step],
            recv_sem=recv_sem.at[step],
            device_id=device(source),
            device_id_type=pl.DeviceIdType.MESH,
        ).wait_recv()
    for copy in copies:
        copy.wait_send()


def push(blocks, axes, call_id, spread=False):
    count = 1
    for axis in axes:
        count *= lax.axis_size(axis)
    shape = (count,) + blocks.shape if spread else blocks.shape
    moved = 2 * blocks.size * blocks.dtype.itemsize
    return pl.pallas_call(
        functools.partial(push_kernel, axes, spread),
        out_shape=jax.ShapeDtypeStruct(shape, blocks.dtype),
        in_specs=[pl.BlockSpec(memory_space=pltpu.VMEM)],
        out_specs=pl.BlockSpec(memory_space=pltpu.VMEM),
        scratch_shapes=[
            pltpu.SemaphoreType.DMA((count,)),
            pltpu.SemaphoreType.DMA((count,)),
            pltpu.SemaphoreType.DMA,
        ],
        cost_estimate=pl.CostEstimate(flops=0, bytes_accessed=moved, transcendentals=0),
        compiler_params=pltpu.CompilerParams(collective_id=call_id, has_side_effects=True),
        name="push_%d" % call_id,
    )(blocks)


def nth_match(table, wanted, places):
    matched = (table == wanted).astype(jnp.int32)
    ranking = jnp.cumsum(matched, axis=1) - 1
    return (matched[:, None, :] == 1) & (ranking[:, None, :] == places[None, :, None])


def arrival_places(new_owner):
    groups = lax.axis_size("grp")
    ranks = lax.axis_size("kv")
    per_dev = new_owner.shape[1] // ranks
    owners = new_owner.reshape(groups * ranks, per_dev)
    myself = lax.axis_index("grp") * ranks + lax.axis_index("kv")
    mine = lax.dynamic_index_in_dim(owners, myself, 0, keepdims=False)
    order = jnp.arange(per_dev, dtype=jnp.int32)
    src_grp = mine // ranks
    earlier = (src_grp[:, None] == src_grp[None, :]) & (order[:, None] < order[None, :])
    before = jnp.sum(earlier.astype(jnp.int32), axis=0)
    return src_grp * NPR + before


def move_pages(kv_pool, new_owner, new_local, gate):
    groups = lax.axis_size("grp")
    ranks = lax.axis_size("kv")
    per_dev = new_owner.shape[1] // ranks
    cap = groups * NPR // ranks
    grp_rank = lax.axis_index("grp")
    kv_rank = lax.axis_index("kv")
    myself = grp_rank * ranks + kv_rank
    places = jnp.arange(cap, dtype=jnp.int32)
    by_col = (
        new_owner.reshape(groups, ranks, per_dev)
        .transpose(1, 0, 2)
        .reshape(ranks, groups * per_dev)
    )
    local_col = (
        new_local.reshape(groups, ranks, per_dev)
        .transpose(1, 0, 2)
        .reshape(ranks, groups * per_dev)
    )
    select = nth_match(by_col, myself, places)
    picked = jnp.sum(jnp.where(select, local_col[:, None, :], 0), axis=2)
    outgoing = jnp.take(kv_pool, picked.reshape(-1), axis=0, mode="clip")
    outgoing, gate = lax.optimization_barrier((outgoing, gate))
    received = lax.all_to_all(outgoing, "kv", split_axis=0, concat_axis=0, tiled=True)
    row_here = lax.dynamic_index_in_dim(by_col, kv_rank, 0, keepdims=False)
    sources = grp_rank * ranks + jnp.arange(ranks, dtype=jnp.int32)
    hits = nth_match(
        jnp.broadcast_to(row_here[None, :], (ranks, row_here.shape[0])), sources[:, None], places
    )
    spots = jnp.arange(row_here.shape[0], dtype=jnp.int32)
    where_f = jnp.sum(jnp.where(hits, spots[None, None, :], 0), axis=2).reshape(-1)
    dest_grp = where_f // per_dev
    dest_pos = where_f % per_dev
    same = (dest_grp[:, None] == dest_grp[None, :]) & (dest_pos[:, None] < dest_pos[None, :])
    rank_in = jnp.sum(same.astype(jnp.int32), axis=0)
    target = dest_grp * NPR + rank_in
    items = jnp.arange(target.shape[0], dtype=jnp.int32)
    inverse = jnp.sum(jnp.where(target[None, :] == items[:, None], items[None, :], 0), axis=1)
    sorted_pages = jnp.take(received, inverse, axis=0, mode="clip")
    return sorted_pages, gate


def page_partials(picked, pages, filled):
    count = pages.shape[0]
    tokens = pages.shape[2]
    kv_here = pages.shape[3] // HEAD_DIM
    ratio = HEADS // KV_HEADS
    keys = pages[:, 0].astype(jnp.float32).reshape(count, tokens, kv_here, HEAD_DIM)
    values = pages[:, 1].astype(jnp.float32).reshape(count, tokens, kv_here, HEAD_DIM)
    picked = picked.reshape(count, kv_here, ratio, HEAD_DIM)
    scores = jnp.einsum("ikgd,itkd->ikgt", picked, keys, precision=lax.Precision.HIGHEST)
    usable = (jnp.arange(tokens, dtype=jnp.int32)[None, :] < filled[:, None])[:, None, None, :]
    scores = jnp.where(usable, scores, neg_fill)
    page_top = jnp.max(scores, axis=3)
    weights = jnp.where(usable, jnp.exp(scores - page_top[..., None]), 0.0)
    page_sum = jnp.sum(weights, axis=3)
    page_acc = jnp.einsum("ikgt,itkd->ikgd", weights, values, precision=lax.Precision.HIGHEST)
    heads_here = kv_here * ratio
    return (
        page_top.reshape(count, heads_here),
        page_sum.reshape(count, heads_here),
        page_acc.reshape(count, heads_here, HEAD_DIM),
    )


def lanes(values, width):
    return jnp.pad(values, [(0, 0)] * (values.ndim - 1) + [(0, width - values.shape[-1])])


def per_device(
    hidden_states,
    attn_gain,
    mlp_gain,
    w_query,
    w_out,
    w_gate,
    w_up,
    w_down,
    kv_pool,
    resident_cache,
    resident_slot,
    resident_len,
    new_owner,
    new_local,
    new_slot,
    new_len,
    token_kv,
):
    groups = lax.axis_size("grp")
    ranks = lax.axis_size("kv")
    pairs = lax.axis_size("tp")
    kv_rank = lax.axis_index("kv")
    tp_rank = lax.axis_index("tp")
    exact = lax.Precision.HIGHEST
    features = hidden_states.astype(jnp.float32)
    slots = features.shape[0]
    width = w_query.shape[1]
    heads_here = width // HEAD_DIM
    kv_here = token_kv.shape[2] // HEAD_DIM
    ratio = HEADS // KV_HEADS
    arrived_at = arrival_places(new_owner)
    partial_query = jnp.dot(
        (features * attn_gain).astype(jnp.bfloat16), w_query, preferred_element_type=jnp.float32
    )
    squares = jnp.sum(features * features, axis=1, keepdims=True)
    shares = jnp.concatenate(
        [partial_query, jnp.broadcast_to(squares, (slots, HEAD_DIM))], axis=1
    ).reshape(ranks, slots // ranks, width + HEAD_DIM)
    shares = jnp.sum(push(shares, ("kv",), 1), axis=0)
    attn_scale = lax.rsqrt(shares[:, width : width + 1] / D + norm_eps)
    query = push(shares[:, :width] * attn_scale * HEAD_DIM ** (-0.5), ("kv",), 2, True)
    query = query.reshape(slots, heads_here, HEAD_DIM)

    items = jnp.arange(arrived_at.shape[0], dtype=jnp.int32)
    hit = arrived_at[None, :] == items[:, None]
    slot_by = jnp.sum(jnp.where(hit, new_slot, 0), axis=1)
    len_by = jnp.sum(jnp.where(hit, new_len, 0), axis=1)
    res_slot = resident_slot[0]
    asked = jnp.take(query, slot_by, axis=0, mode="clip").reshape(groups, NPR * heads_here, HEAD_DIM)
    lens = jnp.broadcast_to(
        len_by.astype(jnp.float32).reshape(groups, NPR, 1), (groups, NPR, HEAD_DIM)
    )
    note_rows = 2 * NPR
    asked = push(jnp.concatenate([asked, lens, jnp.zeros_like(lens)], axis=1), ("grp",), 3)
    sorted_pages, (asked, query) = move_pages(kv_pool, new_owner, new_local, (asked, query))
    body = NPR * heads_here
    len_here = asked[:, body : body + NPR, 0].astype(jnp.int32).reshape(-1)
    far = page_partials(
        asked[:, :body].reshape(groups * NPR, heads_here, HEAD_DIM), sorted_pages, len_here
    )
    answer = jnp.concatenate(
        [
            far[2].reshape(groups, body, HEAD_DIM),
            lanes(far[0], HEAD_DIM).reshape(groups, NPR, HEAD_DIM),
            lanes(far[1], HEAD_DIM).reshape(groups, NPR, HEAD_DIM),
        ],
        axis=1,
    )
    answer = push(answer, ("grp",), 4)
    sorted_pages, answer = lax.optimization_barrier((sorted_pages, answer))
    arrived = lax.all_to_all(sorted_pages, "grp", split_axis=0, concat_axis=0, tiled=True)
    near = page_partials(
        jnp.take(query, res_slot, axis=0, mode="clip"), resident_cache[0], resident_len[0]
    )
    far_count = groups * NPR
    page_top = jnp.concatenate(
        [near[0], answer[:, body : body + NPR, :heads_here].reshape(far_count, heads_here)]
    )
    page_sum = jnp.concatenate(
        [
            near[1],
            answer[:, body + NPR : body + note_rows, :heads_here].reshape(far_count, heads_here),
        ]
    )
    page_acc = jnp.concatenate(
        [near[2], answer[:, :body].reshape(far_count, heads_here, HEAD_DIM)]
    )
    owner_slot = jnp.concatenate([res_slot, slot_by])
    count = owner_slot.shape[0]
    member = owner_slot[None, :] == jnp.arange(slots, dtype=jnp.int32)[:, None]
    slot_top = jnp.max(jnp.where(member[:, :, None], page_top[None], neg_fill), axis=1)
    same = owner_slot[None, :] == owner_slot[:, None]
    reach = jnp.max(jnp.where(same[:, :, None], page_top[None], neg_fill), axis=1)
    fade = jnp.exp(page_top - reach)
    member_f = member.astype(jnp.float32)
    span = HEAD_DIM // ranks
    part = heads_here * span
    faded = (page_acc * fade[..., None]).reshape(count, heads_here, ranks, span)
    faded = faded.transpose(0, 2, 1, 3).reshape(count, ranks * part)
    both = jnp.dot(
        member_f, jnp.concatenate([faded, page_sum * fade], axis=1), precision=exact
    )
    stats = lanes(jnp.concatenate([slot_top, both[:, ranks * part :]], axis=1), HEAD_DIM)
    parts = jnp.stack(
        [
            jnp.concatenate([both[:, rank * part : (rank + 1) * part], stats], axis=1)
            for rank in range(ranks)
        ]
    )
    parts = push(parts, ("kv",), 5)

    own_keys = token_kv[:, 0].astype(jnp.float32).reshape(slots, kv_here, 1, HEAD_DIM)
    grouped = query.reshape(slots, kv_here, ratio, HEAD_DIM)
    own_score = jnp.sum(grouped * own_keys, axis=3).reshape(slots, heads_here)
    tops = parts[:, :, part : part + heads_here]
    sums = parts[:, :, part + heads_here : part + 2 * heads_here]
    top = jnp.maximum(jnp.max(tops, axis=0), own_score)
    fades = jnp.exp(tops - top[None])
    own_weight = jnp.exp(own_score - top)
    total = jnp.sum(sums * fades, axis=0) + own_weight
    lane = jnp.arange(part, dtype=jnp.int32)
    widen = (
        jnp.arange(heads_here, dtype=jnp.int32)[:, None] == (lane // span)[None, :]
    ).astype(jnp.float32)
    factors = jnp.concatenate([fades / total[None], (own_weight / total)[None]], axis=0)
    factors = jnp.dot(
        factors.reshape((ranks + 1) * slots, heads_here), widen, precision=exact
    ).reshape(ranks + 1, slots, part)
    wanted = (lane // (span * ratio)) * HEAD_DIM + kv_rank * span + lane % span
    choose = (
        jnp.arange(kv_here * HEAD_DIM, dtype=jnp.int32)[:, None] == wanted[None, :]
    ).astype(jnp.bfloat16)
    own_piece = jnp.dot(token_kv[:, 1], choose, preferred_element_type=jnp.float32)
    piece = jnp.sum(parts[:, :, :part] * factors[:ranks], axis=0) + own_piece * factors[ranks]
    branch = jnp.dot(
        piece.astype(jnp.bfloat16),
        w_out.reshape(part, w_out.shape[2]),
        preferred_element_type=jnp.float32,
    )
    width_here = features.shape[1]
    column = jnp.arange(ranks * width_here, dtype=jnp.int32)
    mine = (column // width_here == kv_rank) & (tp_rank == 0)
    branch = branch + jnp.where(mine[None, :], jnp.tile(features, (1, ranks)), 0.0)
    row_count = slots // (ranks * pairs)
    blocks = (ranks * pairs, row_count, ranks * width_here)
    laid = push(branch.astype(jnp.bfloat16).reshape(blocks), ("kv", "tp"), 6)
    kept = jnp.sum(laid.astype(jnp.float32), axis=0).astype(jnp.bfloat16)
    resid = push(kept, ("kv", "tp"), 7, True).reshape(slots, ranks * width_here)
    resid_f = resid.astype(jnp.float32)
    mlp_scale = lax.rsqrt(jnp.sum(resid_f * resid_f, axis=1) / D + norm_eps)
    normed_mlp = (resid_f * mlp_gain).astype(jnp.bfloat16)
    gate = jnp.dot(normed_mlp, w_gate, preferred_element_type=jnp.float32) * mlp_scale[:, None]
    upward = jnp.dot(normed_mlp, w_up, preferred_element_type=jnp.float32) * mlp_scale[:, None]
    hidden_units = (jax.nn.silu(gate) * upward).astype(jnp.bfloat16)
    down = jnp.dot(hidden_units, w_down, preferred_element_type=jnp.float32)
    down = push(down.astype(jnp.bfloat16).reshape(blocks), ("kv", "tp"), 8)
    down = jnp.sum(down.astype(jnp.float32), axis=0)
    mixed = (kept.astype(jnp.float32) + down).astype(jnp.bfloat16)
    new_pages = jnp.take(arrived, arrived_at, axis=0, mode="clip")
    return (mixed, new_pages[None])


def solution(mesh):
    return jax.shard_map(
        per_device,
        mesh=mesh,
        in_specs=(
            P("grp", "kv"),
            P("kv"),
            P(),
            P("kv", "tp"),
            P("tp", "kv", None),
            P(None, ("kv", "tp")),
            P(None, ("kv", "tp")),
            P(("kv", "tp"), None),
            P(("grp", "kv"), None, None, "tp"),
            P("grp", "kv", None, None, "tp"),
            P("grp", "kv"),
            P("grp", "kv"),
            P(),
            P(),
            P("grp", "kv"),
            P("grp", "kv"),
            P("grp", None, "tp"),
        ),
        out_specs=(P(("grp", "kv", "tp"), None), P("grp", "kv", None, None, "tp")),
        check_vma=False,
    )
```

profile of v0, /device:TPU:0, one launch (start us, length us, event | category | flops | bytes accessed | tf_op | source)
XLA Modules:
  0.0 276.3 jit_solution(13854043163395884816)
XLA Ops:
  4.9 3.0 %fusion.20 = f32[128,2048]{1,0:T(8,128)S(1)} fusion(bf16[1024,2048]{1,0:T(8,128)(2,1)} %param.20, f32[1024]{0:T(1024)} %param.18, bf16[128,1024]{1,0:T(8,128)(2,1)} %param.17), kind=kOutput, calls=%fused_computation.45 | convolution fusion | flops 537264128 | bytes 5509120 | tf_op jit(solution)/shard_map/dot_general | solution.py:218
  9.1 19.2 %push_1.1 = f32[4,32,2176]{2,1,0:T(8,128)} custom-call(f32[4,32,2176]{2,1,0:T(8,128)} %bitcast.130), custom_call_target="tpu_custom_call" | custom-call | bytes 2228224 | tf_op jit(solution)/shard_map/push_1/pallas_call | solution.py:81
  30.5 16.8 %push_2.1 = f32[4,32,2048]{2,1,0:T(8,128)} custom-call(f32[32,2048]{1,0:T(8,128)} %fusion.22.src), custom_call_target="tpu_custom_call" | custom-call | bytes 524288 | tf_op jit(solution)/shard_map/push_2/pallas_call | solution.py:81
  50.3 8.4 %push_3.1 = f32[4,72,128]{2,1,0:T(8,128)} custom-call(f32[4,72,128]{2,1,0:T(8,128)} %maximum_maximum_fusion.src), custom_call_target="tpu_custom_call" | custom-call | bytes 294912 | tf_op jit(solution)/shard_map/push_3/pallas_call | solution.py:81
  59.4 5.0 %gather_fusion = bf16[16,2,128,512]{3,2,1,0:T(8,128)(2,1)} fusion(bf16[16,2,128,512]{3,2,1,0:T(8,128)(2,1)} %param.25, s32[1024]{0:T(1024)S(1)} %pad_clamp_fusion.4), kind=kCustom, calls=%fused_computation | custom fusion | bytes 8388672 | tf_op jit(solution)/shard_map/jit(_take)/gather | solution.py:138
  64.4 5.2 %all-to-all-start = ((bf16[16,2,128,512]{3,2,1,0:T(8,128)(2,1)}), bf16[16,2,128,512]{3,2,1,0:T(8,128)(2,1)}, u32[]{:S(2)}, u32[]{:S(2)}) async-start(bf16[16,2,128,512]{3,2,1,0:T(8,128)(2,1)} %gather_fusion), calls=%async_computation | async-start | bytes 8388608 | tf_op jit(solution)/shard_map/all_to_all | solution.py:140
  69.7 3.0 %copy.167 = bf16[1,8,2,128,512]{3,4,1,2,0:T(8,128)(2,1)S(1)} copy(bf16[1,8,2,128,512]{4,3,2,1,0:T(8,128)(2,1)} %param.26) | data formatting | bytes 4194304 | tf_op args[9]
  72.7 1.5 fusion.72
  74.8 2.2 fusion.77
  77.1 3.0 %fusion.37 = f32[8,4,4,128]{3,2,1,0:T(4,128)S(1)} fusion(bf16[8,128,4,128]{1,3,2,0:T(8,128)(2,1)} %bitcast.142, f32[8,4,4,128]{3,2,1,0:T(4,128)S(1)} %get-tuple-element.43, f32[8,4,4]{2,1,0:T(4,128)S(1)} %get-tuple-element.42, pred[8,128]{1,0:T(8,128)(4,1)S(1)} %iota_compare_fusion.13), kind=kOutput, calls=%fused_computation.78 | convolution fusion | flops 25198592 | bytes 1181184 | tf_op jit(solution)/shard_map/ikgt,itkd->ikgd/dot_general | solution.py:173
  81.6 3.0 %copy.207 = f32[16,8,4,1024]{3,1,2,0:T(8,128)} copy(f32[16,8,4,1024]{3,2,1,0:T(4,128)S(1)} %bitcast.125) | data formatting | bytes 4194304
  86.8 28.5 %all-to-all-done = bf16[16,2,128,512]{3,2,1,0:T(8,128)(2,1)} async-done(((bf16[16,2,128,512]{3,2,1,0:T(8,128)(2,1)}), bf16[16,2,128,512]{3,2,1,0:T(8,128)(2,1)}, u32[]{:S(2)}, u32[]{:S(2)}) %all-to-all-start) | async-done | bytes 4194336 | tf_op jit(solution)/shard_map/all_to_all | solution.py:140
  115.3 5.0 %gather_fusion.3 = bf16[16,2,128,512]{3,2,1,0:T(8,128)(2,1)} fusion(bf16[16,2,128,512]{3,2,1,0:T(8,128)(2,1)} %all-to-all-done, s32[1024]{0:T(1024)S(1)} %pad_clamp_fusion.1), kind=kCustom, calls=%fused_computation.3 | custom fusion | bytes 8388672 | tf_op jit(solution)/shard_map/jit(_take)/gather | solution.py:155
  120.3 4.6 %fusion.71 = (bf16[16,1,128,512]{3,2,1,0:T(8,128)(2,1)}, bf16[16,1,128,512]{3,2,1,0:T(8,128)(2,1)}) fusion(bf16[16,2,128,512]{3,2,1,0:T(8,128)(2,1)} %gather_fusion.3), kind=kLoop, calls=%fused_computation.185 | loop fusion | bytes 8388608 | tf_op jit(solution)/shard_map/slice | solution.py:165
  124.9 3.0 %copy.170 = bf16[16,1,128,512]{2,3,0,1:T(8,128)(2,1)S(1)} copy(bf16[16,1,128,512]{3,2,1,0:T(8,128)(2,1)} %get-tuple-element.21) | data formatting | bytes 4194304 | tf_op jit(solution)/shard_map/slice | solution.py:164
  127.9 4.0 %copy.172 = bf16[16,1,128,512]{2,3,0,1:T(8,128)(2,1)} copy(bf16[16,1,128,512]{3,2,1,0:T(8,128)(2,1)} %get-tuple-element.20) | data formatting | bytes 4194304 | tf_op jit(solution)/shard_map/slice | solution.py:165
  131.9 1.8 fusion.76
  134.1 5.0 %fusion.31 = f32[16,4,4,128]{3,2,1,0:T(4,128)S(1)} fusion(bf16[16,128,4,128]{1,3,2,0:T(8,128)(2,1)} %bitcast.138, f32[16,4,4,128]{3,2,1,0:T(4,128)S(1)} %get-tuple-element.41, f32[16,4,4]{2,1,0:T(4,128)S(1)} %get-tuple-element.40, pred[16,128]{1,0:T(8,128)(4,1)S(1)} %iota_compare_fusion.7), kind=kOutput, calls=%fused_computation.70 | convolution fusion | flops 50397184 | bytes 2362368 | tf_op jit(solution)/shard_map/ikgt,itkd->ikgd/dot_general | solution.py:173
  140.1 8.2 %push_4.1 = f32[4,72,128]{2,1,0:T(8,128)} custom-call(f32[4,72,128]{2,1,0:T(8,128)} %pad_maximum_fusion.3.src), custom_call_target="tpu_custom_call" | custom-call | bytes 294912 | tf_op jit(solution)/shard_map/push_4/pallas_call | solution.py:81
  154.2 17.1 %push_5.1 = f32[4,128,640]{2,1,0:T(8,128)} custom-call(f32[4,128,640]{2,1,0:T(8,128)} %pad_maximum_fusion.src), custom_call_target="tpu_custom_call" | custom-call | bytes 2621440 | tf_op jit(solution)/shard_map/push_5/pallas_call | solution.py:81
  173.5 5.0 %all-to-all-start.1 = ((bf16[16,2,128,512]{3,2,1,0:T(8,128)(2,1)}), bf16[16,2,128,512]{3,2,1,0:T(8,128)(2,1)}, u32[]{:S(2)}, u32[]{:S(2)}) async-start(bf16[16,2,128,512]{3,2,1,0:T(8,128)(2,1)} %gather_fusion.3), calls=%async_computation.1 | async-start | bytes 8388608 | tf_op jit(solution)/shard_map/all_to_all | solution.py:257
  182.1 4.4 %fusion = bf16[128,4096]{1,0:T(8,128)(2,1)} fusion(bf16[512,4096]{1,0:T(8,128)(2,1)} %bitcast.134, f32[128,4096]{1,0:T(8,128)S(1)} %bitcast.126, f32[128,512]{1,0:T(8,128)} %multiply_reduce_fusion.1, pred[4096]{0:T(1024)(128)(4,1)S(1)} %fusion.50, s32[512]{0:T(512)S(1)} %fusion.61, f32[640,512]{1,0:T(8,128)} %copy-done.2, ...), kind=kOutput, calls=%fused_computation.6 | convolution fusion | flops 606011392 | bytes 8132608 | tf_op jit(solution)/shard_map/dot_general | solution.py:321
  186.6 15.6 %push_6.1 = bf16[8,16,4096]{2,1,0:T(8,128)(2,1)} custom-call(bf16[8,16,4096]{2,1,0:T(8,128)(2,1)} %bitcast.131), custom_call_target="tpu_custom_call" | custom-call | bytes 2097152 | tf_op jit(solution)/shard_map/push_6/pallas_call | solution.py:81
  202.2 2.1 reduce_sum.181.src
  204.2 17.0 %push_7.1 = bf16[8,16,4096]{2,1,0:T(8,128)(2,1)} custom-call(bf16[16,4096]{1,0:T(8,128)(2,1)} %reduce_sum.181.src), custom_call_target="tpu_custom_call" | custom-call | bytes 262144 | tf_op jit(solution)/shard_map/push_7/pallas_call | solution.py:81
  221.2 1.5 multiply_reduce_fusion
  222.8 1.4 fusion.3
  224.3 7.3 %convolution_multiply_fusion.1 = f32[128,1792]{1,0:T(8,128)S(1)} fusion(bf16[128,4096]{1,0:T(8,128)(2,1)S(1)} %fusion.3, bf16[4096,1792]{1,0:T(8,128)(2,1)} %param.22, f32[128]{0:T(128)S(1)} %rsqrt.15), kind=kOutput, calls=%fused_computation.9 | convolution fusion | flops 1879277568 | bytes 16646656 | tf_op jit(solution)/shard_map/dot_general | solution.py:338
  231.5 14.8 %convolution_convert_fusion = bf16[128,4096]{1,0:T(8,128)(2,1)} fusion(bf16[1792,4096]{1,0:T(8,128)(2,1)} %param.24, bf16[128,4096]{1,0:T(8,128)(2,1)S(1)} %fusion.3, bf16[4096,1792]{1,0:T(8,128)(2,1)} %param.23, f32[128,1792]{1,0:T(8,128)S(1)} %convolution_multiply_fusion.1, f32[128]{0:T(128)S(1)} %rsqrt.15), kind=kOutput, calls=%fused_computation.7 | convolution fusion | flops 3760226304 | bytes 32375296 | tf_op jit(solution)/shard_map/dot_general | solution.py:341
  246.3 17.0 %push_8.1 = bf16[8,16,4096]{2,1,0:T(8,128)(2,1)} custom-call(bf16[8,16,4096]{2,1,0:T(8,128)(2,1)} %bitcast.140), custom_call_target="tpu_custom_call" | custom-call | bytes 2097152 | tf_op jit(solution)/shard_map/push_8/pallas_call | solution.py:81
  265.4 5.9 %all-to-all-done.1 = bf16[16,2,128,512]{3,2,1,0:T(8,128)(2,1)} async-done(((bf16[16,2,128,512]{3,2,1,0:T(8,128)(2,1)}), bf16[16,2,128,512]{3,2,1,0:T(8,128)(2,1)}, u32[]{:S(2)}, u32[]{:S(2)}) %all-to-all-start.1) | async-done | bytes 4194336 | tf_op jit(solution)/shard_map/all_to_all | solution.py:257
  271.3 5.0 %gather_fusion.4 = bf16[16,2,128,512]{3,2,1,0:T(8,128)(2,1)} fusion(bf16[16,2,128,512]{3,2,1,0:T(8,128)(2,1)} %all-to-all-done.1, s32[1024]{0:T(1024)S(1)} %pad_clamp_fusion), kind=kCustom, calls=%fused_computation.4 | custom fusion | bytes 8388672 | tf_op jit(solution)/shard_map/jit(_take)/gather | solution.py:345
  (137 shorter events, 30.7 us)
Async XLA Ops:
  30.5 28.5 %copy-start.8 = (s32[4,64]{1,0:T(4,128)S(1)}, s32[4,64]{1,0:T(4,128)}, u32[]{:S(2)}) copy-start(s32[4,64]{1,0:T(4,128)} %param.30) | copy-start | bytes 3076
  64.4 5.2 %copy-start.9 = (s32[1,8]{1,0:T(1,128)S(1)}, s32[1,8]{1,0:T(1,128)}, u32[]{:S(2)}) copy-start(s32[1,8]{1,0:T(1,128)} %param.27) | copy-start | bytes 100
  64.4 5.2 %copy-start.10 = (s32[1,8]{1,0:T(1,128)S(1)}, s32[1,8]{1,0:T(1,128)}, u32[]{:S(2)}) copy-start(s32[1,8]{1,0:T(1,128)} %param.28) | copy-start | bytes 100
  64.4 50.9 %all-to-all-start = ((bf16[16,2,128,512]{3,2,1,0:T(8,128)(2,1)}), bf16[16,2,128,512]{3,2,1,0:T(8,128)(2,1)}, u32[]{:S(2)}, u32[]{:S(2)}) async-start(bf16[16,2,128,512]{3,2,1,0:T(8,128)(2,1)} %gather_fusion), calls=%async_computation | async-start | bytes 8388608 | tf_op jit(solution)/shard_map/all_to_all | solution.py:140
  74.2 6.1 %copy-start.6 = (f32[4,72,128]{2,1,0:T(8,128)S(1)}, f32[4,72,128]{2,1,0:T(8,128)}, u32[]{:S(2)}) copy-start(f32[4,72,128]{2,1,0:T(8,128)} %push_3.1) | copy-start | bytes 442372
  74.2 6.8 %copy-start.3 = (bf16[128,1024]{1,0:T(8,128)(2,1)S(1)}, bf16[128,1024]{1,0:T(8,128)(2,1)}, u32[]{:S(2)}) copy-start(bf16[128,1024]{1,0:T(8,128)(2,1)} %param.17) | copy-start | bytes 786436
  81.6 3.4 %copy-start.5 = (bf16[128,2,512]{2,1,0:T(2,128)(2,1)S(1)}, bf16[128,2,512]{2,1,0:T(2,128)(2,1)}, u32[]{:S(2)}) copy-start(bf16[128,2,512]{2,1,0:T(2,128)(2,1)} %param.33) | copy-start | bytes 786436
  127.9 4.0 %slice-start = ((f32[4,72,128]{2,1,0:T(8,128)}), f32[4,64,128]{2,1,0:T(8,128)S(1)}, s32[]{:S(2)}) async-start(f32[4,72,128]{2,1,0:T(8,128)} %push_3.1), calls=%async_computation.2 | async-start | bytes 262144 | tf_op jit(solution)/shard_map/slice | solution.py:245
  173.5 5.0 %copy-start = (f32[4,128,640]{2,1,0:T(8,128)S(1)}, f32[4,128,640]{2,1,0:T(8,128)}, u32[]{:S(2)}) copy-start(f32[4,128,640]{2,1,0:T(8,128)} %push_5.1) | copy-start | bytes 3932164
  173.5 97.7 %all-to-all-start.1 = ((bf16[16,2,128,512]{3,2,1,0:T(8,128)(2,1)}), bf16[16,2,128,512]{3,2,1,0:T(8,128)(2,1)}, u32[]{:S(2)}, u32[]{:S(2)}) async-start(bf16[16,2,128,512]{3,2,1,0:T(8,128)(2,1)} %gather_fusion.3), calls=%async_computation.1 | async-start | bytes 8388608 | tf_op jit(solution)/shard_map/all_to_all | solution.py:257
  179.4 1.1 copy-start.2
  180.5 1.7 copy-start.1
  202.2 20.7 %copy-start.7 = (f32[4096]{0:T(1024)S(1)}, f32[4096]{0:T(1024)}, u32[]{:S(2)}) copy-start(f32[4096]{0:T(1024)} %param.19) | copy-start | bytes 49156
  246.3 18.4 %copy-start.4 = (bf16[16,4096]{1,0:T(8,128)(2,1)S(1)}, bf16[16,4096]{1,0:T(8,128)(2,1)}, u32[]{:S(2)}) copy-start(bf16[16,4096]{1,0:T(8,128)(2,1)} %reduce_sum.181.src) | copy-start | bytes 393220
where the time goes:
time: 278 us; the launch traced here: 276 us
  Pallas kernels  119 us (43%)
  local copies, waits for them, and re-layouts  45.8 us (16%)
  matrix products  43.2 us (16%)
  waiting for transfers between devices  34.4 us (12%)
  other arithmetic  22.3 us (8%)
  starting transfers between devices  10.2 us (4%)
    pallas_call x8, Pallas kernels, push(): pl.pallas_call(functools.partial(push_kernel, axes, spread), out_shape=ja...  119 us
    all_to_all x1, waiting for transfers between devices, move_pages(): lax.all_to_all(outgoing, 'kv', split_axis=0, concat_axis=0, tiled=True)  28.5 us
    dot_general x1, matrix products, per_device(): down = jnp.dot(hidden_units, w_down, preferred_element_type=jnp.float32)  14.8 us
    slice x3, local copies, waits for them, and re-layouts, page_partials(): pages[:, 1].astype(jnp.float32).reshape(count, tokens, kv_here, HEAD_DIM)  10 us
    unnamed x31, local copies, waits for them, and re-layouts  9.96 us
    dot_general x2, matrix products, page_partials(): jnp.einsum('ikgt,itkd->ikgd', weights, values, precision=lax.Precision.HI...  7.99 us
    dot_general x1, matrix products, per_device(): jnp.dot(normed_mlp, w_gate, preferred_element_type=jnp.float32)  7.25 us
    all_to_all x1, waiting for transfers between devices, per_device(): lax.all_to_all(sorted_pages, 'grp', split_axis=0, concat_axis=0, tiled=True)  5.89 us
  transfers between devices with their start and end apart: 2, of which 2 were waited for; matrix products, arithmetic and copies ran while one was open for 19% of the time, Pallas kernels for 18%

commit v1 on v0

v1 whole, which is shorter than its diff:
```python
import functools

import jax
import jax.numpy as jnp
from jax import lax
from jax.experimental import pallas as pl
from jax.experimental.pallas import tpu as pltpu
from jax.sharding import PartitionSpec as P

D = 4096
HEADS = 32
KV_HEADS = 8
HEAD_DIM = 128
NPR = 4


neg_fill = -1e30
norm_eps = 1e-05


def push_kernel(axes, spread, src, out, send_sem, recv_sem, own_sem):
    sizes = [lax.axis_size(axis) for axis in axes]
    count = 1
    me = jnp.int32(0)
    for axis, size in zip(axes, sizes):
        me = me * size + lax.axis_index(axis)
        count *= size

    def device(index):
        where = {}
        for axis, size in reversed(list(zip(axes, sizes))):
            where[axis] = lax.rem(index, size)
            index = index // size
        return where

    barrier = pltpu.get_barrier_semaphore()
    for step in range(1, count):
        pl.semaphore_signal(
            barrier,
            inc=1,
            device_id=device(lax.rem(me + step, count)),
            device_id_type=pl.DeviceIdType.MESH,
        )
    pl.semaphore_wait(barrier, count - 1)
    copies = []
    for step in range(1, count):
        peer = lax.rem(me + step, count)
        copy = pltpu.make_async_remote_copy(
            src_ref=src if spread else src.at[peer],
            dst_ref=out.at[me],
            send_sem=send_sem.at[step],
            recv_sem=recv_sem.at[step],
            device_id=device(peer),
            device_id_type=pl.DeviceIdType.MESH,
        )
        copy.start()
        copies.append(copy)
    own = pltpu.make_async_copy(src if spread else src.at[me], out.at[me], own_sem)
    own.start()
    own.wait()
    for step in range(1, count):
        source = lax.rem(me - step + count, count)
        pltpu.make_async_remote_copy(
            src_ref=src if spread else src.at[source],
            dst_ref=out.at[source],
            send_sem=send_sem.at[step],
            recv_sem=recv_sem.at[step],
            device_id=device(source),
            device_id_type=pl.DeviceIdType.MESH,
        ).wait_recv()
    for copy in copies:
        copy.wait_send()


def push(blocks, axes, call_id, spread=False):
    count = 1
    for axis in axes:
        count *= lax.axis_size(axis)
    shape = (count,) + blocks.shape if spread else blocks.shape
    moved = 2 * blocks.size * blocks.dtype.itemsize
    return pl.pallas_call(
        functools.partial(push_kernel, axes, spread),
        out_shape=jax.ShapeDtypeStruct(shape, blocks.dtype),
        in_specs=[pl.BlockSpec(memory_space=pltpu.VMEM)],
        out_specs=pl.BlockSpec(memory_space=pltpu.VMEM),
        scratch_shapes=[
            pltpu.SemaphoreType.DMA((count,)),
            pltpu.SemaphoreType.DMA((count,)),
            pltpu.SemaphoreType.DMA,
        ],
        cost_estimate=pl.CostEstimate(flops=0, bytes_accessed=moved, transcendentals=0),
        compiler_params=pltpu.CompilerParams(collective_id=call_id, has_side_effects=True),
        name="push_%d" % call_id,
    )(blocks)


def nth_match(table, wanted, places):
    matched = (table == wanted).astype(jnp.int32)
    ranking = jnp.cumsum(matched, axis=1) - 1
    return (matched[:, None, :] == 1) & (ranking[:, None, :] == places[None, :, None])


def arrival_places(new_owner):
    groups = lax.axis_size("grp")
    ranks = lax.axis_size("kv")
    per_dev = new_owner.shape[1] // ranks
    owners = new_owner.reshape(groups * ranks, per_dev)
    myself = lax.axis_index("grp") * ranks + lax.axis_index("kv")
    mine = lax.dynamic_index_in_dim(owners, myself, 0, keepdims=False)
    order = jnp.arange(per_dev, dtype=jnp.int32)
    src_grp = mine // ranks
    earlier = (src_grp[:, None] == src_grp[None, :]) & (order[:, None] < order[None, :])
    before = jnp.sum(earlier.astype(jnp.int32), axis=0)
    return src_grp * NPR + before


def lanes(values, width):
    return jnp.pad(values, [(0, 0)] * (values.ndim - 1) + [(0, width - values.shape[-1])])


NEAR_ROWS = 8


def split2(x):
    high = x.astype(jnp.bfloat16)
    return high, (x - high.astype(jnp.float32)).astype(jnp.bfloat16)


def split3(x):
    high = x.astype(jnp.bfloat16)
    rest = x - high.astype(jnp.float32)
    middle = rest.astype(jnp.bfloat16)
    return high, middle, (rest - middle.astype(jnp.float32)).astype(jnp.bfloat16)


def mm(a, b):
    return jnp.dot(a, b, preferred_element_type=jnp.float32)


def mm_nt(a, b):
    return lax.dot_general(a, b, (((1,), (1,)), ((), ())), preferred_element_type=jnp.float32)


def rows_of(shape):
    return lax.broadcasted_iota(jnp.int32, shape, 0)


def lanes_of(shape):
    return lax.broadcasted_iota(jnp.int32, shape, 1)


def half_turn(x):
    return pltpu.roll(x, 4, 0)


def fold(tile, odd):
    if tile.shape[1] < 256:
        return tile
    half = tile.shape[1] // 2
    low, high = tile[:, :half], tile[:, half:]
    top = rows_of(low.shape) < 4
    if odd:
        return jnp.where(top, half_turn(low), high)
    return jnp.where(top, low, half_turn(high))


def pick_rows(first, second, odd):
    first = jnp.where(odd, half_turn(first), first)
    second = jnp.where(odd, second, half_turn(second))
    return jnp.where(rows_of(first.shape) < 4, first, second)


def unfold(first, second, width, odd):
    if width < 256:
        return pick_rows(first, second, odd)
    top = rows_of(first.shape) < 4
    low = jnp.where(top, first, half_turn(second))
    high = jnp.where(top, half_turn(first), second)
    return jnp.concatenate([low, high], axis=1)


def column_of(row, offset):
    wide = jnp.broadcast_to(row, (8, 128)).astype(jnp.float32)
    hit = lanes_of((8, 128)) == rows_of((8, 128)) + offset
    return jnp.sum(jnp.where(hit, wide, 0.0), axis=1, keepdims=True)


def place_in_group(groups, ranks):
    grp = lax.axis_index("grp")
    kv = lax.axis_index("kv")
    me = grp * ranks + kv

    def flat(index):
        return {"grp": index // ranks, "kv": lax.rem(index, ranks)}

    return grp, kv, me, flat


def front_kernel(
    dims,
    picked,
    inverse,
    meta,
    hidden,
    gain,
    token_keys,
    token_values,
    wq_hbm,
    pool_hbm,
    res_hbm,
    wo_hbm,
    branch_out,
    sorted_out,
    pool_v,
    send_v,
    recv_v,
    sorted_v,
    res_v,
    wq_v,
    wo_v,
    meta_v,
    qpart,
    qrecv,
    ss_send,
    ss_recv,
    onehot,
    onehot_t,
    near_q_send,
    near_q_recv,
    far_q_send,
    far_q_recv,
    own_t,
    own_send,
    own_recv,
    near_acc,
    near_lse,
    far_acc,
    far_lse,
    near_a_send,
    near_a_recv,
    near_l_send,
    near_l_recv,
    far_a_send,
    far_a_recv,
    far_l_send,
    far_l_recv,
    all_lse,
    all_acc,
    load_sem,
    meta_ss,
    meta_rs,
    page_ss,
    page_rs,
    q_ss,
    q_rs,
    s_ss,
    s_rs,
    nq_ss,
    nq_rs,
    fq_ss,
    fq_rs,
    own_ss,
    own_rs,
    na_ss,
    na_rs,
    nl_ss,
    nl_rs,
    fa_ss,
    fa_rs,
    fl_ss,
    fl_rs,
    out_sem,
):
    groups, ranks, cap, kv_here, heads = (dims[name] for name in ("groups", "ranks", "cap", "kv_here", "heads"))
    ratio = heads // kv_here
    hg = heads // ranks
    hgw = hg * HEAD_DIM
    span = HEAD_DIM // ranks
    part = heads * span
    per_tile = HEAD_DIM // span
    rep = HEAD_DIM // heads
    everyone = groups * ranks
    tiles = groups * NPR // 8
    count_tiles = ranks + ranks * tiles
    grp, kv, me, flat = place_in_group(groups, ranks)
    odd_here = lax.rem(grp, 2) == 1
    slots = hidden.shape[0]

    def kv_peer(step):
        return lax.rem(kv + step, ranks)

    def kv_from(step):
        return lax.rem(kv - step + ranks, ranks)

    def all_peer(step):
        return lax.rem(me + step, everyone)

    def all_from(step):
        return lax.rem(me - step + everyone, everyone)

    pending = []

    def remote(src, dst, ss, rs, where):
        copy = pltpu.make_async_remote_copy(
            src_ref=src,
            dst_ref=dst,
            send_sem=ss,
            recv_sem=rs,
            device_id=where,
            device_id_type=pl.DeviceIdType.MESH,
        )
        copy.start()
        pending.append(copy)

    def arrive(src, dst, ss, rs, where):
        pltpu.make_async_remote_copy(
            src_ref=src,
            dst_ref=dst,
            send_sem=ss,
            recv_sem=rs,
            device_id=where,
            device_id_type=pl.DeviceIdType.MESH,
        ).wait_recv()

    loads = []
    for c in range(kv_here):
        cols = pl.ds(c * HEAD_DIM, HEAD_DIM)
        loads.append(
            pltpu.make_async_copy(pool_hbm.at[:, :, :, cols], pool_v[c], load_sem.at[c])
        )
    load_q = pltpu.make_async_copy(wq_hbm, wq_v, load_sem.at[kv_here])
    load_r = pltpu.make_async_copy(res_hbm, res_v, load_sem.at[kv_here + 1])
    load_o = pltpu.make_async_copy(wo_hbm, wo_v, load_sem.at[kv_here + 2])
    loads[0].start()
    load_q.start()
    for copy in loads[1:]:
        copy.start()
    load_r.start()
    load_o.start()

    barrier = pltpu.get_barrier_semaphore()
    for step in range(1, everyone):
        pl.semaphore_signal(
            barrier, inc=1, device_id=flat(all_peer(step)), device_id_type=pl.DeviceIdType.MESH
        )
    pl.semaphore_wait(barrier, everyone - 1)

    for step in range(1, everyone):
        remote(meta, meta_v.at[me], meta_ss.at[step], meta_rs.at[step], flat(all_peer(step)))
    meta_v[me] = meta[...]

    def send_pages(c):
        loads[c].wait()

        def pick(i, carry):
            for a in range(cap):
                where = i * cap + a
                target = lax.rem(kv + i, ranks) * cap + a
                send_v[c][where] = pool_v[c][picked[target]]
            return carry

        for a in range(cap):
            recv_v[c][kv * cap + a] = pool_v[c][picked[kv * cap + a]]
        lax.fori_loop(1, ranks, pick, 0)
        for step in range(1, ranks):
            remote(
                send_v[c].at[pl.ds(step * cap, cap)],
                recv_v[c].at[pl.ds(kv * cap, cap)],
                page_ss.at[c, step],
                page_rs.at[c, step],
                {"kv": kv_peer(step)},
            )

    send_pages(0)

    load_q.wait()
    features = hidden[...].astype(jnp.float32)
    normed = (features * gain[...]).astype(jnp.bfloat16)
    for j in range(ranks):
        qpart[j] = mm(normed, wq_v[:, j * hgw : (j + 1) * hgw])
    squares = jnp.sum(features * features, axis=1, keepdims=True)
    ss_send[...] = jnp.transpose(jnp.broadcast_to(squares, (slots, 128)))[:8]
    ss_recv[kv] = ss_send[...]
    for step in range(1, ranks):
        peer = kv_peer(step)
        remote(ss_send, ss_recv.at[kv], s_ss.at[step], s_rs.at[step], {"kv": peer})
        remote(qpart.at[peer], qrecv.at[kv], q_ss.at[step], q_rs.at[step], {"kv": peer})

    for step in range(1, everyone):
        source = all_from(step)
        arrive(meta, meta_v.at[source], meta_ss.at[step], meta_rs.at[step], flat(source))
    slot_rows = []
    for k in range(ranks):
        slot_rows.append(column_of(meta_v[grp * ranks + k][2:3], 0))
    for k in range(ranks):
        for t in range(tiles):
            slot_rows.append(column_of(meta_v[grp * ranks + k][0:1], 8 * t))
    for i, column in enumerate(slot_rows):
        onehot[8 * i : 8 * i + 8, :] = (
            column == lanes_of((8, slots)).astype(jnp.float32)
        ).astype(jnp.float32)
    for i in range(8 * count_tiles, onehot.shape[0], 8):
        onehot[i : i + 8, :] = jnp.zeros((8, slots), jnp.float32)

    send_pages(1)

    for step in range(1, ranks):
        source = kv_from(step)
        arrive(ss_send, ss_recv.at[source], s_ss.at[step], s_rs.at[step], {"kv": source})
        arrive(
            qpart.at[source], qrecv.at[source], q_ss.at[step], q_rs.at[step], {"kv": source}
        )
    total_ss = ss_recv[0]
    for j in range(1, ranks):
        total_ss = total_ss + ss_recv[j]
    total_ss = jnp.transpose(jnp.broadcast_to(total_ss[0:1], (128, slots)))
    scale = lax.rsqrt(total_ss / D + norm_eps) * HEAD_DIM ** (-0.5)
    pieces = []
    for i in range(hg):
        cols = slice(i * HEAD_DIM, (i + 1) * HEAD_DIM)
        piece = qpart[kv, :, cols]
        for step in range(1, ranks):
            piece = piece + qrecv[kv_from(step), :, cols]
        pieces.append(piece * scale)
    kv_head = (kv * hg) // ratio
    own_key = token_keys[:, pl.ds(pl.multiple_of(kv_head * HEAD_DIM, HEAD_DIM), HEAD_DIM)]
    own_key = own_key.astype(jnp.float32)
    lane_head = lanes_of((slots, 128)) // rep
    own = jnp.zeros((slots, 128), jnp.float32)
    for i in range(hg):
        score = jnp.sum(pieces[i] * own_key, axis=1, keepdims=True)
        own = jnp.where(lane_head == kv * hg + i, score, own)
    own_t[...] = jnp.transpose(own)
    own_send[...] = own_t[pl.ds(pl.multiple_of(kv * (hg * rep), 8), hg * rep), :]
    own_recv[kv] = own_send[...]
    hot = onehot[...].astype(jnp.bfloat16)
    chosen = []
    for piece in pieces:
        high, middle, low = split3(piece)
        chosen.append(mm(hot, high) + mm(hot, middle) + mm(hot, low))
    chosen = jnp.concatenate(chosen, axis=1)
    for k in range(ranks):
        near_q_send[k] = chosen[8 * k : 8 * k + 8]
        for t in range(tiles):
            at = 8 * (ranks + k * tiles + t)
            tile = chosen[at : at + 8]
            far_q_send[(2 * t) * ranks + k] = fold(tile, False)
            far_q_send[(2 * t + 1) * ranks + k] = fold(tile, True)
    near_q_recv[kv] = near_q_send[kv]
    far_q_recv[me] = far_q_send[me]
    for step in range(1, ranks):
        peer = kv_peer(step)
        remote(
            near_q_send.at[peer], near_q_recv.at[kv], nq_ss.at[step], nq_rs.at[step], {"kv": peer}
        )
        remote(own_send, own_recv.at[kv], own_ss.at[step], own_rs.at[step], {"kv": peer})
    for step in range(1, everyone):
        peer = all_peer(step)
        remote(
            far_q_send.at[peer], far_q_recv.at[me], fq_ss.at[step], fq_rs.at[step], flat(peer)
        )

    for c in range(2, kv_here):
        send_pages(c)

    row_id = rows_of((8, 128))
    row_masks = [
        jnp.concatenate([(row_id == p).astype(jnp.bfloat16)] * ratio, axis=0) for p in range(8)
    ]

    def page_tile(queries, keys, values, lengths):
        q_high, q_middle, q_low = split3(jnp.concatenate(queries, axis=0))
        rows = 8 * ratio
        scores = jnp.zeros((3 * rows, HEAD_DIM), jnp.float32)
        for p in range(8):
            mask = row_masks[p]
            stacked = jnp.concatenate([q_high * mask, q_middle * mask, q_low * mask], axis=0)
            scores = scores + mm_nt(stacked, keys(p))
        scores = scores[:rows] + scores[rows : 2 * rows] + scores[2 * rows :]
        usable = lanes_of((rows, 128)).astype(jnp.float32) < jnp.concatenate(
            [lengths] * ratio, axis=0
        )
        scores = jnp.where(usable, scores, neg_fill)
        top = jnp.max(scores, axis=1, keepdims=True)
        weights = jnp.where(usable, jnp.exp(scores - top), 0.0)
        total = jnp.sum(weights, axis=1, keepdims=True)
        w_high, w_low = split2(weights)
        acc = jnp.zeros((2 * rows, HEAD_DIM), jnp.float32)
        for p in range(8):
            mask = row_masks[p]
            stacked = jnp.concatenate([w_high * mask, w_low * mask], axis=0)
            acc = acc + mm(stacked, values(p))
        acc = (acc[:rows] + acc[rows:]) / total
        return acc, top + jnp.log(total)

    lane_id = lanes_of((8, 128))

    def pack_acc(load, k):
        columns = []
        for first in range(0, heads, per_tile):
            merged = None
            for i in range(per_tile):
                turn = (span * (i - k)) % HEAD_DIM
                moved = load(first + i)
                if turn:
                    moved = pltpu.roll(moved, turn, 1)
                merged = moved if merged is None else jnp.where(lane_id // span == i, moved, merged)
            columns.append(merged)
        return columns[0] if len(columns) == 1 else jnp.concatenate(columns, axis=1)

    for step in range(1, ranks):
        source = kv_from(step)
        arrive(
            near_q_send.at[source],
            near_q_recv.at[source],
            nq_ss.at[step],
            nq_rs.at[step],
            {"kv": source},
        )
    load_r.wait()
    near_length = column_of(meta[3:4], 0)
    lse_tile = jnp.zeros((8, 128), jnp.float32)
    for j in range(kv_here):
        queries = []
        for i in range(ratio):
            head = j * ratio + i
            at = (head % hg) * HEAD_DIM
            queries.append(near_q_recv[head // hg, :, at : at + HEAD_DIM])
        cols = slice(j * HEAD_DIM, (j + 1) * HEAD_DIM)
        acc, lse = page_tile(
            queries,
            lambda p: res_v[p, 0, :, cols],
            lambda p: res_v[p, 1, :, cols],
            near_length,
        )
        for i in range(ratio):
            head = j * ratio + i
            near_acc[head] = acc[8 * i : 8 * i + 8]
            lse_tile = jnp.where(lane_id // rep == head, lse[8 * i : 8 * i + 8], lse_tile)
    near_l_send[...] = lse_tile
    near_l_recv[kv] = lse_tile
    for k in range(ranks):
        near_a_send[k] = pack_acc(lambda head: near_acc[head], k)
    near_a_recv[kv] = near_a_send[kv]
    for step in range(1, ranks):
        peer = kv_peer(step)
        remote(near_l_send, near_l_recv.at[kv], nl_ss.at[step], nl_rs.at[step], {"kv": peer})
        remote(
            near_a_send.at[peer], near_a_recv.at[kv], na_ss.at[step], na_rs.at[step], {"kv": peer}
        )

    for step in range(1, everyone):
        source = all_from(step)
        arrive(
            far_q_send.at[source],
            far_q_recv.at[source],
            fq_ss.at[step],
            fq_rs.at[step],
            flat(source),
        )
    far_lengths = []
    for t in range(tiles):
        offset = grp * NPR
        first = column_of(meta_v[(2 * t) * ranks + kv][1:2], offset)
        second = column_of(meta_v[(2 * t + 1) * ranks + kv][1:2], offset - 4)
        far_lengths.append(jnp.where(rows_of((8, 1)) < 4, first, second))
    far_lse_tiles = [jnp.zeros((8, 128), jnp.float32) for _ in range(tiles)]
    stores = []
    for c in range(kv_here):
        for step in range(1, ranks):
            source = kv_from(step)
            arrive(
                send_v[c].at[pl.ds(step * cap, cap)],
                recv_v[c].at[pl.ds(source * cap, cap)],
                page_ss.at[c, step],
                page_rs.at[c, step],
                {"kv": source},
            )

        def sort(i, carry):
            sorted_v[c][i] = recv_v[c][inverse[i]]
            return carry

        lax.fori_loop(0, groups * NPR, sort, 0)
        cols = pl.ds(c * HEAD_DIM, HEAD_DIM)
        store = pltpu.make_async_copy(
            sorted_v[c], sorted_out.at[:, :, :, cols], out_sem.at[c]
        )
        store.start()
        stores.append(store)
        for t in range(tiles):
            queries = []
            for i in range(ratio):
                head = c * ratio + i
                k = head // hg
                wide = unfold(
                    far_q_recv[(2 * t) * ranks + k],
                    far_q_recv[(2 * t + 1) * ranks + k],
                    hgw,
                    odd_here,
                )
                at = (head % hg) * HEAD_DIM
                queries.append(wide[:, at : at + HEAD_DIM])
            acc, lse = page_tile(
                queries,
                lambda p: sorted_v[c][8 * t + p, 0],
                lambda p: sorted_v[c][8 * t + p, 1],
                far_lengths[t],
            )
            for i in range(ratio):
                head = c * ratio + i
                far_acc[t, head] = acc[8 * i : 8 * i + 8]
                far_lse_tiles[t] = jnp.where(
                    lane_id // rep == head, lse[8 * i : 8 * i + 8], far_lse_tiles[t]
                )
    for t in range(tiles):
        for k in range(ranks):
            tile = pack_acc(lambda head: far_acc[t, head], k)
            far_a_send[(2 * t) * ranks + k] = fold(tile, False)
            far_a_send[(2 * t + 1) * ranks + k] = fold(tile, True)
        far_l_send[t] = far_lse_tiles[t]
    far_a_recv[me] = far_a_send[me]
    far_l_recv[me] = far_l_send[grp // 2]
    for step in range(1, everyone):
        peer = all_peer(step)
        remote(
            far_l_send.at[peer // (2 * ranks)],
            far_l_recv.at[me],
            fl_ss.at[step],
            fl_rs.at[step],
            flat(peer),
        )
        remote(
            far_a_send.at[peer], far_a_recv.at[me], fa_ss.at[step], fa_rs.at[step], flat(peer)
        )

    onehot_t[...] = jnp.transpose(onehot[...]).astype(jnp.bfloat16)
    lane = lanes_of((1, part))
    wanted = (lane // (span * ratio)) * HEAD_DIM + kv * span + lax.rem(lane, span)
    choose = (rows_of((kv_here * HEAD_DIM, part)) == wanted).astype(jnp.bfloat16)
    own_piece = mm(token_values[...], choose)
    widen = (
        rows_of((128, part)) == (lanes_of((128, part)) // span) * rep
    ).astype(jnp.bfloat16)
    for step in range(1, ranks):
        source = kv_from(step)
        arrive(own_send, own_recv.at[source], own_ss.at[step], own_rs.at[step], {"kv": source})
        arrive(
            near_l_send, near_l_recv.at[source], nl_ss.at[step], nl_rs.at[step], {"kv": source}
        )
        arrive(
            near_a_send.at[source],
            near_a_recv.at[source],
            na_ss.at[step],
            na_rs.at[step],
            {"kv": source},
        )
    own_all = jnp.transpose(own_recv[...].reshape(128, slots))
    for k in range(ranks):
        all_lse[8 * k : 8 * k + 8, :] = near_l_recv[k]
        all_acc[8 * k : 8 * k + 8, :] = near_a_recv[k]
    for step in range(1, everyone):
        source = all_from(step)
        arrive(
            far_l_send.at[0],
            far_l_recv.at[source],
            fl_ss.at[step],
            fl_rs.at[step],
            flat(source),
        )
        arrive(
            far_a_send.at[source],
            far_a_recv.at[source],
            fa_ss.at[step],
            fa_rs.at[step],
            flat(source),
        )
    for k in range(ranks):
        for t in range(tiles):
            at = 8 * (ranks + k * tiles + t)
            one, two = (2 * t) * ranks + k, (2 * t + 1) * ranks + k
            all_lse[at : at + 8, :] = pick_rows(far_l_recv[one], far_l_recv[two], odd_here)
            all_acc[at : at + 8, :] = unfold(far_a_recv[one], far_a_recv[two], part, odd_here)
    used = 8 * count_tiles
    for at in range(used, all_lse.shape[0], 8):
        all_lse[at : at + 8, :] = jnp.zeros((8, 128), jnp.float32)
        all_acc[at : at + 8, :] = jnp.zeros((8, part), jnp.float32)
    top = jnp.full((slots, 128), neg_fill, jnp.float32)
    slot_id = rows_of((slots, 128)).astype(jnp.float32)
    diagonal = lax.rem(lane_id, rep)
    turns = [(row_id == diagonal + rep * h).astype(jnp.float32) for h in range(8 // rep if rep < 8 else 1)]
    for i, column in enumerate(slot_rows):
        tile = all_lse[8 * i : 8 * i + 8, :]
        for hit in turns:
            value = jnp.sum(tile * hit, axis=0, keepdims=True)
            owner = jnp.sum(column * hit, axis=0, keepdims=True)
            top = jnp.maximum(top, jnp.where(slot_id == owner, value, neg_fill))
    wide_lane = lanes_of((slots, 128))
    shift = 1
    while shift < rep:
        up = pltpu.roll(top, shift, 1)
        down = pltpu.roll(top, 128 - shift, 1)
        top = jnp.maximum(top, jnp.where((wide_lane & shift) != 0, up, down))
        shift *= 2
    top = jnp.maximum(top, own_all)
    high, middle, low = split3(top)
    page_top = mm(hot, high) + mm(hot, middle) + mm(hot, low)
    page_weight = jnp.exp(all_lse[...] - page_top)
    own_weight = jnp.exp(own_all - top)
    hot_t = onehot_t[...]
    high, low = split2(page_weight)
    total = mm(hot_t, high) + mm(hot_t, low) + own_weight
    high, low = split2(
        jnp.concatenate([page_weight, own_weight, pl.reciprocal(total)], axis=0)
    )
    spread = mm(high, widen) + mm(low, widen)
    padded = all_lse.shape[0]
    high, low = split2(all_acc[...] * spread[:padded])
    gathered = mm(hot_t, high) + mm(hot_t, low)
    gathered = gathered + own_piece * spread[padded : padded + slots]
    piece = (gathered * spread[padded + slots :]).astype(jnp.bfloat16)
    load_o.wait()
    columns = branch_out.shape[1]
    for at in range(0, columns, 512):
        branch_out[:, at : at + 512] = mm(piece, wo_v[:, at : at + 512])
    for store in stores:
        store.wait()
    for copy in pending:
        copy.wait_send()


def front(dims, picked, inverse, meta, hidden, gain, token_keys, token_values, wq, pool, res, wo):
    groups, ranks, cap, kv_here, heads = (dims[name] for name in ("groups", "ranks", "cap", "kv_here", "heads"))
    hgw = heads // ranks * HEAD_DIM
    part = heads * HEAD_DIM // ranks
    everyone = groups * ranks
    pages = groups * NPR
    tiles = pages // 8
    slots = hidden.shape[0]
    rep = HEAD_DIM // heads
    tokens = pool.shape[2]
    rows = 8 * (ranks + ranks * tiles)
    rows = -(-rows // 128) * 128
    half = lambda width: width // 2 if width >= 256 else width
    f32, bf16 = jnp.float32, jnp.bfloat16
    chunk = lambda count: [pltpu.VMEM((count, 2, tokens, HEAD_DIM), bf16) for _ in range(kv_here)]
    dma = lambda *shape: pltpu.SemaphoreType.DMA(shape)
    scratch = [
        chunk(pool.shape[0]),
        chunk(pages),
        chunk(pages),
        chunk(pages),
        pltpu.VMEM(res.shape, bf16),
        pltpu.VMEM(wq.shape, bf16),
        pltpu.VMEM(wo.shape, bf16),
        pltpu.VMEM((everyone, 8, 128), jnp.int32),
        pltpu.VMEM((ranks, slots, hgw), f32),
        pltpu.VMEM((ranks, slots, hgw), f32),
        pltpu.VMEM((8, slots), f32),
        pltpu.VMEM((ranks, 8, slots), f32),
        pltpu.VMEM((rows, slots), f32),
        pltpu.VMEM((slots, rows), bf16),
        pltpu.VMEM((ranks, 8, hgw), f32),
        pltpu.VMEM((ranks, 8, hgw), f32),
        pltpu.VMEM((everyone, 8, half(hgw)), f32),
        pltpu.VMEM((everyone, 8, half(hgw)), f32),
        pltpu.VMEM((128, slots), f32),
        pltpu.VMEM((heads // ranks * rep, slots), f32),
        pltpu.VMEM((ranks, heads // ranks * rep, slots), f32),
        pltpu.VMEM((heads, 8, HEAD_DIM), f32),
        pltpu.VMEM((8, 128), f32),
        pltpu.VMEM((tiles, heads, 8, HEAD_DIM), f32),
        pltpu.VMEM((tiles, 8, 128), f32),
        pltpu.VMEM((ranks, 8, part), f32),
        pltpu.VMEM((ranks, 8, part), f32),
        pltpu.VMEM((8, 128), f32),
        pltpu.VMEM((ranks, 8, 128), f32),
        pltpu.VMEM((everyone, 8, half(part)), f32),
        pltpu.VMEM((everyone, 8, half(part)), f32),
        pltpu.VMEM((tiles, 8, 128), f32),
        pltpu.VMEM((everyone, 8, 128), f32),
        pltpu.VMEM((rows, 128), f32),
        pltpu.VMEM((rows, part), f32),
        dma(kv_here + 3),
        dma(everyone),
        dma(everyone),
        dma(kv_here, ranks),
        dma(kv_here, ranks),
        dma(ranks),
        dma(ranks),
        dma(ranks),
        dma(ranks),
        dma(ranks),
        dma(ranks),
        dma(everyone),
        dma(everyone),
        dma(ranks),
        dma(ranks),
        dma(ranks),
        dma(ranks),
        dma(ranks),
        dma(ranks),
        dma(everyone),
        dma(everyone),
        dma(everyone),
        dma(everyone),
        dma(kv_here),
    ]
    vmem = pl.BlockSpec(memory_space=pltpu.VMEM)
    smem = pl.BlockSpec(memory_space=pltpu.SMEM)
    hbm = pl.BlockSpec(memory_space=pl.ANY)
    return pl.pallas_call(
        functools.partial(front_kernel, dims),
        out_shape=(
            jax.ShapeDtypeStruct((slots, wo.shape[1]), f32),
            jax.ShapeDtypeStruct((pages,) + pool.shape[1:], bf16),
        ),
        in_specs=[smem, smem, vmem, vmem, vmem, vmem, vmem, hbm, hbm, hbm, hbm],
        out_specs=(vmem, hbm),
        scratch_shapes=scratch,
        compiler_params=pltpu.CompilerParams(
            collective_id=1, has_side_effects=True, vmem_limit_bytes=60 << 20
        ),
        name="front",
    )(picked, inverse, meta, hidden, gain, token_keys, token_values, wq, pool, res, wo)


def route_tables(new_owner, new_local):
    groups = lax.axis_size("grp")
    ranks = lax.axis_size("kv")
    per_dev = new_owner.shape[1] // ranks
    cap = groups * NPR // ranks
    grp_rank = lax.axis_index("grp")
    kv_rank = lax.axis_index("kv")
    myself = grp_rank * ranks + kv_rank
    places = jnp.arange(cap, dtype=jnp.int32)
    by_col = (
        new_owner.reshape(groups, ranks, per_dev)
        .transpose(1, 0, 2)
        .reshape(ranks, groups * per_dev)
    )
    local_col = (
        new_local.reshape(groups, ranks, per_dev)
        .transpose(1, 0, 2)
        .reshape(ranks, groups * per_dev)
    )
    select = nth_match(by_col, myself, places)
    picked = jnp.sum(jnp.where(select, local_col[:, None, :], 0), axis=2)
    row_here = lax.dynamic_index_in_dim(by_col, kv_rank, 0, keepdims=False)
    sources = grp_rank * ranks + jnp.arange(ranks, dtype=jnp.int32)
    hits = nth_match(
        jnp.broadcast_to(row_here[None, :], (ranks, row_here.shape[0])), sources[:, None], places
    )
    spots = jnp.arange(row_here.shape[0], dtype=jnp.int32)
    where_f = jnp.sum(jnp.where(hits, spots[None, None, :], 0), axis=2).reshape(-1)
    dest_grp = where_f // per_dev
    dest_pos = where_f % per_dev
    same = (dest_grp[:, None] == dest_grp[None, :]) & (dest_pos[:, None] < dest_pos[None, :])
    rank_in = jnp.sum(same.astype(jnp.int32), axis=0)
    target = dest_grp * NPR + rank_in
    items = jnp.arange(target.shape[0], dtype=jnp.int32)
    inverse = jnp.sum(jnp.where(target[None, :] == items[:, None], items[None, :], 0), axis=1)
    return picked.reshape(-1), inverse


def per_device(
    hidden_states,
    attn_gain,
    mlp_gain,
    w_query,
    w_out,
    w_gate,
    w_up,
    w_down,
    kv_pool,
    resident_cache,
    resident_slot,
    resident_len,
    new_owner,
    new_local,
    new_slot,
    new_len,
    token_kv,
):
    groups = lax.axis_size("grp")
    ranks = lax.axis_size("kv")
    pairs = lax.axis_size("tp")
    kv_rank = lax.axis_index("kv")
    tp_rank = lax.axis_index("tp")
    features = hidden_states.astype(jnp.float32)
    slots = features.shape[0]
    heads_here = w_query.shape[1] // HEAD_DIM
    kv_here = token_kv.shape[2] // HEAD_DIM
    dims = {
        "groups": groups,
        "ranks": ranks,
        "cap": groups * NPR // ranks,
        "kv_here": kv_here,
        "heads": heads_here,
    }
    arrived_at = arrival_places(new_owner)
    picked, inverse = route_tables(new_owner, new_local)
    items = jnp.arange(arrived_at.shape[0], dtype=jnp.int32)
    hit = arrived_at[None, :] == items[:, None]
    slot_by = jnp.sum(jnp.where(hit, new_slot, 0), axis=1)
    len_by = jnp.sum(jnp.where(hit, new_len, 0), axis=1)
    meta = jnp.stack(
        [
            lanes(values[None], 128)[0]
            for values in (slot_by, len_by, resident_slot[0], resident_len[0])
        ]
    )
    meta = jnp.pad(meta, ((0, 4), (0, 0)))
    branch, sorted_pages = front(
        dims,
        picked,
        inverse,
        meta,
        hidden_states,
        attn_gain[None],
        token_kv[:, 0],
        token_kv[:, 1],
        w_query,
        kv_pool,
        resident_cache[0],
        w_out.reshape(-1, w_out.shape[2]),
    )
    arrived = lax.all_to_all(sorted_pages, "grp", split_axis=0, concat_axis=0, tiled=True)
    width_here = features.shape[1]
    column = jnp.arange(ranks * width_here, dtype=jnp.int32)
    mine = (column // width_here == kv_rank) & (tp_rank == 0)
    branch = branch + jnp.where(mine[None, :], jnp.tile(features, (1, ranks)), 0.0)
    row_count = slots // (ranks * pairs)
    blocks = (ranks * pairs, row_count, ranks * width_here)
    laid = push(branch.astype(jnp.bfloat16).reshape(blocks), ("kv", "tp"), 6)
    kept = jnp.sum(laid.astype(jnp.float32), axis=0).astype(jnp.bfloat16)
    resid = push(kept, ("kv", "tp"), 7, True).reshape(slots, ranks * width_here)
    resid_f = resid.astype(jnp.float32)
    mlp_scale = lax.rsqrt(jnp.sum(resid_f * resid_f, axis=1) / D + norm_eps)
    normed_mlp = (resid_f * mlp_gain).astype(jnp.bfloat16)
    gate = jnp.dot(normed_mlp, w_gate, preferred_element_type=jnp.float32) * mlp_scale[:, None]
    upward = jnp.dot(normed_mlp, w_up, preferred_element_type=jnp.float32) * mlp_scale[:, None]
    hidden_units = (jax.nn.silu(gate) * upward).astype(jnp.bfloat16)
    down = jnp.dot(hidden_units, w_down, preferred_element_type=jnp.float32)
    down = push(down.astype(jnp.bfloat16).reshape(blocks), ("kv", "tp"), 8)
    down = jnp.sum(down.astype(jnp.float32), axis=0)
    mixed = (kept.astype(jnp.float32) + down).astype(jnp.bfloat16)
    new_pages = jnp.take(arrived, arrived_at, axis=0, mode="clip")
    return (mixed, new_pages[None])


def solution(mesh):
    return jax.shard_map(
        per_device,
        mesh=mesh,
        in_specs=(
            P("grp", "kv"),
            P("kv"),
            P(),
            P("kv", "tp"),
            P("tp", "kv", None),
            P(None, ("kv", "tp")),
            P(None, ("kv", "tp")),
            P(("kv", "tp"), None),
            P(("grp", "kv"), None, None, "tp"),
            P("grp", "kv", None, None, "tp"),
            P("grp", "kv"),
            P("grp", "kv"),
            P(),
            P(),
            P("grp", "kv"),
            P("grp", "kv"),
            P("grp", None, "tp"),
        ),
        out_specs=(P(("grp", "kv", "tp"), None), P("grp", "kv", None, None, "tp")),
        check_vma=False,
    )
```

time: 278 us -> 194 us (0.70)
  local copies, waits for them, and re-layouts: 45.8 us -> 13.3 us
  waiting for transfers between devices: 34.4 us -> 8.91 us
  matrix products: 43.2 us -> 22 us
  Pallas kernels: 119 us -> 132 us
  other arithmetic: 22.3 us -> 11.6 us
  starting transfers between devices: 10.2 us -> 5.17 us
    pallas_call x0 -> x1, Pallas kernels: none -> 81.8 us  [front(): pl.pallas_call(functools.partial(front_kernel, dims), out_shape=(jax.Shap...]
    pallas_call x8 -> x3, Pallas kernels: 119 us -> 49.8 us  [push(): pl.pallas_call(functools.partial(push_kernel, axes, spread), out_shape=ja...]
    all_to_all x1 -> x0, waiting for transfers between devices: 28.5 us -> none  [move_pages(): lax.all_to_all(outgoing, 'kv', split_axis=0, concat_axis=0, tiled=True)]
    dot_general x8 -> x0, matrix products: 21.2 us -> none  [the longest x2 7.99 us: page_partials(): jnp.einsum('ikgt,itkd->ikgd', weights, values, precision=lax.Precision.HI...]
    slice x11 -> x1, local copies, waits for them, and re-layouts: 14.9 us -> 1.48 us  [per_device(): token_kv[:, 1]]
    gather x4 -> x0, local copies, waits for them, and re-layouts: 11.2 us -> none  [the longest x1 5.03 us: move_pages(): outgoing = jnp.take(kv_pool, picked.reshape(-1), axis=0, mode='clip')]
    unnamed x31 -> x9, local copies, waits for them, and re-layouts: 9.96 us -> 1.67 us
    all_to_all x1 -> x0, starting transfers between devices: 5.17 us -> none  [move_pages(): lax.all_to_all(outgoing, 'kv', split_axis=0, concat_axis=0, tiled=True)]
  transfers between devices with their start and end apart: 2 -> 1, of which waited for: 2 -> 1; matrix products, arithmetic and copies ran while one was open for 19% -> 17% of each run, Pallas kernels for 18% -> 26%
where the time goes in v1:
time: 194 us; the launch traced here: 193 us
  Pallas kernels  132 us (68%)
  matrix products  22 us (11%)
  local copies, waits for them, and re-layouts  13.3 us (7%)
  other arithmetic  11.6 us (6%)
  waiting for transfers between devices  8.91 us (5%)
  starting transfers between devices  5.17 us (3%)
    pallas_call x1, Pallas kernels, front(): pl.pallas_call(functools.partial(front_kernel, dims), out_shape=(jax.Shap...  81.8 us
    pallas_call x3, Pallas kernels, push(): pl.pallas_call(functools.partial(push_kernel, axes, spread), out_shape=ja...  49.8 us
    dot_general x1, matrix products, per_device(): down = jnp.dot(hidden_units, w_down, preferred_element_type=jnp.float32)  14.8 us
    all_to_all x1, waiting for transfers between devices, per_device(): lax.all_to_all(sorted_pages, 'grp', split_axis=0, concat_axis=0, tiled=True)  8.91 us
    dot_general x1, matrix products, per_device(): jnp.dot(normed_mlp, w_gate, preferred_element_type=jnp.float32)  7.25 us
    all_to_all x1, starting transfers between devices, per_device(): lax.all_to_all(sorted_pages, 'grp', split_axis=0, concat_axis=0, tiled=True)  5.17 us
    gather x1, local copies, waits for them, and re-layouts, per_device(): new_pages = jnp.take(arrived, arrived_at, axis=0, mode='clip')  5.01 us
  transfers between devices with their start and end apart: 1, of which 1 were waited for; matrix products, arithmetic and copies ran while one was open for 17% of the time, Pallas kernels for 26%

profile of v1, /device:TPU:0, one launch (start us, length us, event | category | flops | bytes accessed | tf_op | source)
XLA Modules:
  0.0 193.5 jit_solution(17181183628302544506)
XLA Ops:
  0.6 0.8 reshape.355
  1.4 0.8 reshape.350
  2.2 0.8 reshape.352
  3.2 0.2 reduce_window_sum.18
  3.5 0.1 select_reduce_fusion.3
  3.8 0.7 select_reduce_fusion.2.inverse
  4.7 0.8 select_reduce_fusion.1
  5.4 0.7 pad_add_fusion
  6.1 0.6 pad.22.meta
  6.7 0.2 reduce_window_sum.17
  7.0 0.1 select_reduce_fusion.4
  7.1 0.6 reshape.353.picked
  7.8 1.5 fusion.16
  9.2 0.7 copy_bitcast_fusion
  10.0 81.8 %front.1 = (f32[128,4096]{1,0:T(8,128)}, bf16[16,2,128,512]{3,2,1,0:T(8,128)(2,1)}) custom-call(s32[16]{0:T(128)} %reshape.353.picked, s32[16]{0:T(128)} %select_reduce_fusion.2.inverse, s32[8,128]{1,0:T(8,128)} %pad.22.meta, bf16[128,1024]{1,0:T(8,128)(2,1)} %hidden.1, f32[1,1024]{1,0:T(1,128)} %bitcast.72, bf16[128,512]{1,0:T(8,128)(2,1)} %get-tuple-element.18.token_keys, ...), custom_call_target="tpu_custom_call" | custom-call | tf_op jit(solution)/shard_map/front/pallas_call | solution.py:812
  91.8 5.2 %all-to-all-start = ((bf16[16,2,128,512]{3,2,1,0:T(8,128)(2,1)}), bf16[16,2,128,512]{3,2,1,0:T(8,128)(2,1)}, u32[]{:S(2)}, u32[]{:S(2)}) async-start(bf16[16,2,128,512]{3,2,1,0:T(8,128)(2,1)} %get-tuple-element.5), calls=%async_computation | async-start | bytes 8388608 | tf_op jit(solution)/shard_map/all_to_all | solution.py:928
  97.0 0.5 tile.4
  97.5 1.7 copy.32
  99.2 1.3 add_convert_fusion
  100.4 15.7 %push_6.1 = bf16[8,16,4096]{2,1,0:T(8,128)(2,1)} custom-call(bf16[8,16,4096]{2,1,0:T(8,128)(2,1)} %bitcast.67), custom_call_target="tpu_custom_call" | custom-call | bytes 2097152 | tf_op jit(solution)/shard_map/push_6/pallas_call | solution.py:81
  116.2 2.1 %reduce_sum.105.src = bf16[16,4096]{1,0:T(8,128)(2,1)} reduce(bf16[8,16,4096]{2,1,0:T(8,128)(2,1)} %push_6.1, bf16[]{:T(256)} %constant.93.clone.1), dimensions={0}, to_apply=%region_9.10 | reduce | flops 458752 | bytes 1179650 | tf_op jit(solution)/shard_map/reduce_sum | solution.py:936
  118.2 17.1 %push_7.1 = bf16[8,16,4096]{2,1,0:T(8,128)(2,1)} custom-call(bf16[16,4096]{1,0:T(8,128)(2,1)} %reduce_sum.105.src), custom_call_target="tpu_custom_call" | custom-call | bytes 262144 | tf_op jit(solution)/shard_map/push_7/pallas_call | solution.py:81
  135.3 1.5 multiply_reduce_fusion
  136.8 0.1 rsqrt.11
  136.9 1.4 fusion.2
  138.4 7.3 %convolution_multiply_fusion.1 = f32[128,1792]{1,0:T(8,128)S(1)} fusion(bf16[128,4096]{1,0:T(8,128)(2,1)S(1)} %fusion.2, bf16[4096,1792]{1,0:T(8,128)(2,1)} %param.22, f32[128]{0:T(128)S(1)} %rsqrt.11), kind=kOutput, calls=%fused_computation.3 | convolution fusion | flops 1879277568 | bytes 16646656 | tf_op jit(solution)/shard_map/dot_general | solution.py:941
  145.6 14.8 %convolution_convert_fusion = bf16[128,4096]{1,0:T(8,128)(2,1)} fusion(bf16[1792,4096]{1,0:T(8,128)(2,1)} %param.24, bf16[128,4096]{1,0:T(8,128)(2,1)S(1)} %fusion.2, bf16[4096,1792]{1,0:T(8,128)(2,1)} %param.23, f32[128,1792]{1,0:T(8,128)S(1)} %convolution_multiply_fusion.1, f32[128]{0:T(128)S(1)} %rsqrt.11), kind=kOutput, calls=%fused_computation.1 | convolution fusion | flops 3760226304 | bytes 32375296 | tf_op jit(solution)/shard_map/dot_general | solution.py:944
  160.4 17.0 %push_8.1 = bf16[8,16,4096]{2,1,0:T(8,128)(2,1)} custom-call(bf16[8,16,4096]{2,1,0:T(8,128)(2,1)} %bitcast.69), custom_call_target="tpu_custom_call" | custom-call | bytes 2097152 | tf_op jit(solution)/shard_map/push_8/pallas_call | solution.py:81
  177.5 1.4 convert_reduce_fusion
  178.9 0.7 add_convert_fusion.1
  179.5 8.9 %all-to-all-done = bf16[16,2,128,512]{3,2,1,0:T(8,128)(2,1)} async-done(((bf16[16,2,128,512]{3,2,1,0:T(8,128)(2,1)}), bf16[16,2,128,512]{3,2,1,0:T(8,128)(2,1)}, u32[]{:S(2)}, u32[]{:S(2)}) %all-to-all-start) | async-done | bytes 4194336 | tf_op jit(solution)/shard_map/all_to_all | solution.py:928
  188.5 5.0 %gather_fusion = bf16[16,2,128,512]{3,2,1,0:T(8,128)(2,1)} fusion(bf16[16,2,128,512]{3,2,1,0:T(8,128)(2,1)} %all-to-all-done, s32[1024]{0:T(1024)S(1)} %pad_clamp_fusion), kind=kCustom, calls=%fused_computation | custom fusion | bytes 8388672 | tf_op jit(solution)/shard_map/jit(_take)/gather | solution.py:948
  (29 shorter events, 0.7 us)
Async XLA Ops:
  91.8 5.2 %copy-start.2 = (bf16[128,1024]{1,0:T(8,128)(2,1)S(1)}, bf16[128,1024]{1,0:T(8,128)(2,1)}, u32[]{:S(2)}) copy-start(bf16[128,1024]{1,0:T(8,128)(2,1)} %hidden.1) | copy-start | bytes 786436
  91.8 96.7 %all-to-all-start = ((bf16[16,2,128,512]{3,2,1,0:T(8,128)(2,1)}), bf16[16,2,128,512]{3,2,1,0:T(8,128)(2,1)}, u32[]{:S(2)}, u32[]{:S(2)}) async-start(bf16[16,2,128,512]{3,2,1,0:T(8,128)(2,1)} %get-tuple-element.5), calls=%async_computation | async-start | bytes 8388608 | tf_op jit(solution)/shard_map/all_to_all | solution.py:928
  96.9 2.2 %copy-start = (f32[128,4096]{1,0:T(8,128)S(1)}, f32[128,4096]{1,0:T(8,128)}, u32[]{:S(2)}) copy-start(f32[128,4096]{1,0:T(8,128)} %get-tuple-element.4) | copy-start | bytes 6291460
  99.2 37.7 %copy-start.3 = (f32[4096]{0:T(1024)S(1)}, f32[4096]{0:T(1024)}, u32[]{:S(2)}) copy-start(f32[4096]{0:T(1024)} %param.19) | copy-start | bytes 49156
  145.6 33.2 %copy-start.1 = (bf16[16,4096]{1,0:T(8,128)(2,1)S(1)}, bf16[16,4096]{1,0:T(8,128)(2,1)}, u32[]{:S(2)}) copy-start(bf16[16,4096]{1,0:T(8,128)(2,1)} %reduce_sum.105.src) | copy-start | bytes 393220

commit v2 on v1

--- a/solution.py
+++ b/solution.py
@@ -16,82 +16,6 @@
 
 neg_fill = -1e30
 norm_eps = 1e-05
-
-
-def push_kernel(axes, spread, src, out, send_sem, recv_sem, own_sem):
-    sizes = [lax.axis_size(axis) for axis in axes]
-    count = 1
-    me = jnp.int32(0)
-    for axis, size in zip(axes, sizes):
-        me = me * size + lax.axis_index(axis)
-        count *= size
-
-    def device(index):
-        where = {}
-        for axis, size in reversed(list(zip(axes, sizes))):
-            where[axis] = lax.rem(index, size)
-            index = index // size
-        return where
-
-    barrier = pltpu.get_barrier_semaphore()
-    for step in range(1, count):
-        pl.semaphore_signal(
-            barrier,
-            inc=1,
-            device_id=device(lax.rem(me + step, count)),
-            device_id_type=pl.DeviceIdType.MESH,
-        )
-    pl.semaphore_wait(barrier, count - 1)
-    copies = []
-    for step in range(1, count):
-        peer = lax.rem(me + step, count)
-        copy = pltpu.make_async_remote_copy(
-            src_ref=src if spread else src.at[peer],
-            dst_ref=out.at[me],
-            send_sem=send_sem.at[step],
-            recv_sem=recv_sem.at[step],
-            device_id=device(peer),
-            device_id_type=pl.DeviceIdType.MESH,
-        )
-        copy.start()
-        copies.append(copy)
-    own = pltpu.make_async_copy(src if spread else src.at[me], out.at[me], own_sem)
-    own.start()
-    own.wait()
-    for step in range(1, count):
-        source = lax.rem(me - step + count, count)
-        pltpu.make_async_remote_copy(
-            src_ref=src if spread else src.at[source],
-            dst_ref=out.at[source],
-            send_sem=send_sem.at[step],
-            recv_sem=recv_sem.at[step],
-            device_id=device(source),
-            device_id_type=pl.DeviceIdType.MESH,
-        ).wait_recv()
-    for copy in copies:
-        copy.wait_send()
-
-
-def push(blocks, axes, call_id, spread=False):
-    count = 1
-    for axis in axes:
-        count *= lax.axis_size(axis)
-    shape = (count,) + blocks.shape if spread else blocks.shape
-    moved = 2 * blocks.size * blocks.dtype.itemsize
-    return pl.pallas_call(
-        functools.partial(push_kernel, axes, spread),
-        out_shape=jax.ShapeDtypeStruct(shape, blocks.dtype),
-        in_specs=[pl.BlockSpec(memory_space=pltpu.VMEM)],
-        out_specs=pl.BlockSpec(memory_space=pltpu.VMEM),
-        scratch_shapes=[
-            pltpu.SemaphoreType.DMA((count,)),
-            pltpu.SemaphoreType.DMA((count,)),
-            pltpu.SemaphoreType.DMA,
-        ],
-        cost_estimate=pl.CostEstimate(flops=0, bytes_accessed=moved, transcendentals=0),
-        compiler_params=pltpu.CompilerParams(collective_id=call_id, has_side_effects=True),
-        name="push_%d" % call_id,
-    )(blocks)
 
 
 def nth_match(table, wanted, places):
@@ -118,7 +42,8 @@
     return jnp.pad(values, [(0, 0)] * (values.ndim - 1) + [(0, width - values.shape[-1])])
 
 
-NEAR_ROWS = 8
+RING = 4
+DOWN_RING = 4
 
 
 def split2(x):
@@ -196,7 +121,7 @@
     return grp, kv, me, flat
 
 
-def front_kernel(
+def step_kernel(
     dims,
     picked,
     inverse,
@@ -209,8 +134,12 @@
     pool_hbm,
     res_hbm,
     wo_hbm,
-    branch_out,
-    sorted_out,
+    mlp_gain,
+    wg_hbm,
+    wu_hbm,
+    wd_hbm,
+    mixed_out,
+    arrived_out,
     pool_v,
     send_v,
     recv_v,
@@ -246,7 +175,26 @@
     far_l_recv,
     all_lse,
     all_acc,
+    piece_v,
+    keep_v,
+    r1_send,
+    r1_recv,
+    r2_send,
+    r2_recv,
+    d1_send,
+    d1_recv,
+    d2_send,
+    d2_recv,
+    kept_v,
+    resid_v,
+    normed_v,
+    units_v,
+    wg_v,
+    wu_v,
+    wd_v,
     load_sem,
+    gate_sem,
+    down_sem,
     meta_ss,
     meta_rs,
     page_ss,
@@ -269,7 +217,21 @@
     fa_rs,
     fl_ss,
     fl_rs,
-    out_sem,
+    z_ss,
+    z_rs,
+    z_own,
+    r1_ss,
+    r1_rs,
+    r2_ss,
+    r2_rs,
+    d1_ss,
+    d1_rs,
+    d2_ss,
+    d2_rs,
+    g_ss,
+    g_rs,
+    gp_ss,
+    gp_rs,
 ):
     groups, ranks, cap, kv_here, heads = (dims[name] for name in ("groups", "ranks", "cap", "kv_here", "heads"))
     ratio = heads // kv_here
@@ -283,6 +245,8 @@
     tiles = groups * NPR // 8
     count_tiles = ranks + ranks * tiles
     grp, kv, me, flat = place_in_group(groups, ranks)
+    tp = lax.axis_index("tp")
+    partner = {"tp": 1 - tp}
     odd_here = lax.rem(grp, 2) == 1
     slots = hidden.shape[0]
 
@@ -343,7 +307,10 @@
         pl.semaphore_signal(
             barrier, inc=1, device_id=flat(all_peer(step)), device_id_type=pl.DeviceIdType.MESH
         )
-    pl.semaphore_wait(barrier, everyone - 1)
+    pl.semaphore_signal(
+        barrier, inc=1, device_id=partner, device_id_type=pl.DeviceIdType.MESH
+    )
+    pl.semaphore_wait(barrier, everyone)
 
     for step in range(1, everyone):
         remote(meta, meta_v.at[me], meta_ss.at[step], meta_rs.at[step], flat(all_peer(step)))
@@ -371,6 +338,53 @@
                 {"kv": kv_peer(step)},
             )
 
+    def sort_pages(c):
+        for step in range(1, ranks):
+            source = kv_from(step)
+            arrive(
+                send_v[c].at[pl.ds(step * cap, cap)],
+                recv_v[c].at[pl.ds(source * cap, cap)],
+                page_ss.at[c, step],
+                page_rs.at[c, step],
+                {"kv": source},
+            )
+
+        def sort(i, carry):
+            sorted_v[c][i] = recv_v[c][inverse[i]]
+            return carry
+
+        lax.fori_loop(0, groups * NPR, sort, 0)
+
+    def pages_of(group):
+        return pl.ds(pl.multiple_of(group * NPR, NPR), NPR)
+
+    def grp_peer(step):
+        return lax.rem(grp + step, groups)
+
+    def grp_from(step):
+        return lax.rem(grp - step + groups, groups)
+
+    stores = []
+
+    def forward_pages(c, kind):
+        cols = pl.ds(c * HEAD_DIM, HEAD_DIM)
+        for step in range(1, groups):
+            peer = grp_peer(step)
+            remote(
+                sorted_v[c].at[pages_of(peer), kind],
+                arrived_out.at[pages_of(grp), kind, :, cols],
+                z_ss.at[c, kind, step],
+                z_rs.at[c, kind, step],
+                {"grp": peer},
+            )
+        store = pltpu.make_async_copy(
+            sorted_v[c].at[pages_of(grp), kind],
+            arrived_out.at[pages_of(grp), kind, :, cols],
+            z_own.at[c, kind],
+        )
+        store.start()
+        stores.append(store)
+
     send_pages(0)
 
     load_q.wait()
@@ -378,6 +392,32 @@
     normed = (features * gain[...]).astype(jnp.bfloat16)
     for j in range(ranks):
         qpart[j] = mm(normed, wq_v[:, j * hgw : (j + 1) * hgw])
+    tile_n = wg_v.shape[2]
+    gate_tiles = wg_hbm.shape[1] // tile_n
+    ring = wg_v.shape[0]
+    cw = wd_v.shape[2]
+    chunks = wd_hbm.shape[1] // cw
+    down_ring = wd_v.shape[0]
+
+    def gate_loads(n):
+        cols = pl.ds(n * tile_n, tile_n)
+        slot = n % ring
+        return (
+            pltpu.make_async_copy(wg_hbm.at[:, cols], wg_v.at[slot], gate_sem.at[0, slot]),
+            pltpu.make_async_copy(wu_hbm.at[:, cols], wu_v.at[slot], gate_sem.at[1, slot]),
+        )
+
+    def down_load(c):
+        slot = c % down_ring
+        return pltpu.make_async_copy(
+            wd_hbm.at[:, pl.ds(c * cw, cw)], wd_v.at[slot], down_sem.at[slot]
+        )
+
+    for n in range(min(ring, gate_tiles)):
+        for copy in gate_loads(n):
+            copy.start()
+    for c in range(min(down_ring, chunks)):
+        down_load(c).start()
     squares = jnp.sum(features * features, axis=1, keepdims=True)
     ss_send[...] = jnp.transpose(jnp.broadcast_to(squares, (slots, 128)))[:8]
     ss_recv[kv] = ss_send[...]
@@ -403,6 +443,9 @@
         onehot[i : i + 8, :] = jnp.zeros((8, slots), jnp.float32)
 
     send_pages(1)
+    sort_pages(0)
+    forward_pages(0, 0)
+    forward_pages(0, 1)
 
     for step in range(1, ranks):
         source = kv_from(step)
@@ -565,29 +608,12 @@
         second = column_of(meta_v[(2 * t + 1) * ranks + kv][1:2], offset - 4)
         far_lengths.append(jnp.where(rows_of((8, 1)) < 4, first, second))
     far_lse_tiles = [jnp.zeros((8, 128), jnp.float32) for _ in range(tiles)]
-    stores = []
     for c in range(kv_here):
-        for step in range(1, ranks):
-            source = kv_from(step)
-            arrive(
-                send_v[c].at[pl.ds(step * cap, cap)],
-                recv_v[c].at[pl.ds(source * cap, cap)],
-                page_ss.at[c, step],
-                page_rs.at[c, step],
-                {"kv": source},
-            )
-
-        def sort(i, carry):
-            sorted_v[c][i] = recv_v[c][inverse[i]]
-            return carry
-
-        lax.fori_loop(0, groups * NPR, sort, 0)
-        cols = pl.ds(c * HEAD_DIM, HEAD_DIM)
-        store = pltpu.make_async_copy(
-            sorted_v[c], sorted_out.at[:, :, :, cols], out_sem.at[c]
-        )
-        store.start()
-        stores.append(store)
+        if c > 0:
+            sort_pages(c)
+        if c == 1:
+            forward_pages(1, 0)
+            forward_pages(1, 1)
         for t in range(tiles):
             queries = []
             for i in range(ratio):
@@ -633,6 +659,10 @@
         remote(
             far_a_send.at[peer], far_a_recv.at[me], fa_ss.at[step], fa_rs.at[step], flat(peer)
         )
+
+    for c in range(2, kv_here):
+        forward_pages(c, 0)
+        forward_pages(c, 1)
 
     onehot_t[...] = jnp.transpose(onehot[...]).astype(jnp.bfloat16)
     lane = lanes_of((1, part))
@@ -719,17 +749,168 @@
     gathered = mm(hot_t, high) + mm(hot_t, low)
     gathered = gathered + own_piece * spread[padded : padded + slots]
     piece = (gathered * spread[padded + slots :]).astype(jnp.bfloat16)
+    piece_v[...] = piece.reshape(piece_v.shape)
+    rows16 = piece_v.shape[2]
+    half = ranks * rows16
+
+    def halves_last(ref):
+        return jnp.concatenate(
+            [ref[:, 1 - tp].reshape(half, part), ref[:, tp].reshape(half, part)], axis=0
+        )
+
+    def scatter_start(c, value, send, recv, ss, rs):
+        send[c] = value[:half].astype(jnp.bfloat16)
+        remote(send.at[c], recv.at[c], ss.at[c], rs.at[c], partner)
+        keep_v[c] = value[half:]
+
+    def scatter_middle(c, extra, first, second, sems1, sems2):
+        arrive(first[0].at[c], first[1].at[c], sems1[0].at[c], sems1[1].at[c], partner)
+        both = keep_v[c] + first[1][c].astype(jnp.float32)
+        if extra is not None:
+            both = both + extra
+        second[0][c] = both.astype(jnp.bfloat16).reshape(ranks, rows16, cw)
+        second[1][c, kv] = second[0][c, kv]
+        for step in range(1, ranks):
+            peer = kv_peer(step)
+            remote(
+                second[0].at[c, peer],
+                second[1].at[c, kv],
+                sems2[0].at[c, step],
+                sems2[1].at[c, step],
+                {"kv": peer},
+            )
+
+    def scatter_end(c, second, sems2):
+        for step in range(1, ranks):
+            source = kv_from(step)
+            arrive(
+                second[0].at[c, source],
+                second[1].at[c, source],
+                sems2[0].at[c, step],
+                sems2[1].at[c, step],
+                {"kv": source},
+            )
+        total = second[1][c, 0].astype(jnp.float32)
+        for j in range(1, ranks):
+            total = total + second[1][c, j].astype(jnp.float32)
+        return total
+
     load_o.wait()
-    columns = branch_out.shape[1]
-    for at in range(0, columns, 512):
-        branch_out[:, at : at + 512] = mm(piece, wo_v[:, at : at + 512])
+    ordered = halves_last(piece_v)
+    width_here = hidden.shape[1]
+    lag = 2
+    for c in range(chunks + lag):
+        if c < chunks:
+            scatter_start(
+                c, mm(ordered, wo_v[:, c * cw : (c + 1) * cw]), r1_send, r1_recv, r1_ss, r1_rs
+            )
+        if c >= lag:
+            d = c - lag
+            at = (d * cw) % width_here
+            mine = hidden[:, at : at + cw].reshape(ranks, 2, rows16, cw)
+            mine = jnp.where(tp == 0, mine[:, 0], mine[:, 1]).reshape(half, cw)
+            mine = mine.astype(jnp.float32)
+            mine = jnp.where(kv == (d * cw) // width_here, mine, 0.0)
+            scatter_middle(
+                d, mine, (r1_send, r1_recv), (r2_send, r2_recv), (r1_ss, r1_rs), (r2_ss, r2_rs)
+            )
+    for c in range(chunks):
+        block = scatter_end(c, (r2_send, r2_recv), (r2_ss, r2_rs)).astype(jnp.bfloat16)
+        kept_v[c] = block
+        resid_v[c, 1, kv] = block
+        for step in range(1, ranks):
+            remote(
+                kept_v.at[c],
+                resid_v.at[c, 1, kv],
+                g_ss.at[c, step],
+                g_rs.at[c, step],
+                {"kv": kv_peer(step)},
+            )
+        remote(kept_v.at[c], resid_v.at[c, 0, kv], gp_ss.at[c, 0], gp_rs.at[c, 0], partner)
+    square_sum = jnp.zeros((2 * half, 1), jnp.float32)
+    for c in range(chunks):
+        for step in range(1, ranks):
+            source = kv_from(step)
+            arrive(
+                kept_v.at[c],
+                resid_v.at[c, 1, source],
+                g_ss.at[c, step],
+                g_rs.at[c, step],
+                {"kv": source},
+            )
+            remote(
+                resid_v.at[c, 1, source],
+                resid_v.at[c, 0, source],
+                gp_ss.at[c, step],
+                gp_rs.at[c, step],
+                partner,
+            )
+    for c in range(chunks):
+        for step in range(ranks):
+            source = kv_from(step)
+            arrive(
+                kept_v.at[c],
+                resid_v.at[c, 0, source],
+                gp_ss.at[c, step],
+                gp_rs.at[c, step],
+                partner,
+            )
+        block = resid_v[c].reshape(2 * half, cw).astype(jnp.float32)
+        square_sum = square_sum + jnp.sum(block * block, axis=1, keepdims=True)
+        cols = slice(c * cw, (c + 1) * cw)
+        normed_v[:, cols] = (block * mlp_gain[:, cols]).astype(jnp.bfloat16)
+    mlp_scale = lax.rsqrt(square_sum / D + norm_eps)
+    for n in range(gate_tiles):
+        slot = n % ring
+        for copy in gate_loads(n):
+            copy.wait()
+        gate = mm(normed_v[...], wg_v[slot]) * mlp_scale
+        upward = mm(normed_v[...], wu_v[slot]) * mlp_scale
+        units = gate / (1.0 + jnp.exp(-gate)) * upward
+        units_v[:, n * tile_n : (n + 1) * tile_n] = units.astype(jnp.bfloat16)
+        if n + ring < gate_tiles:
+            for copy in gate_loads(n + ring):
+                copy.start()
+    for c in range(chunks + lag):
+        if c < chunks:
+            down_load(c).wait()
+            value = mm(units_v[...], wd_v[c % down_ring])
+            scatter_start(c, value, d1_send, d1_recv, d1_ss, d1_rs)
+            if c + down_ring < chunks:
+                down_load(c + down_ring).start()
+        if c >= lag:
+            scatter_middle(
+                c - lag,
+                None,
+                (d1_send, d1_recv),
+                (d2_send, d2_recv),
+                (d1_ss, d1_rs),
+                (d2_ss, d2_rs),
+            )
+    for c in range(chunks):
+        total = scatter_end(c, (d2_send, d2_recv), (d2_ss, d2_rs))
+        total = total + kept_v[c].astype(jnp.float32)
+        mixed_out[:, c * cw : (c + 1) * cw] = total.astype(jnp.bfloat16)
+    for c in range(kv_here):
+        cols = pl.ds(c * HEAD_DIM, HEAD_DIM)
+        for kind in range(2):
+            for step in range(1, groups):
+                source = grp_from(step)
+                arrive(
+                    sorted_v[c].at[pages_of(source), kind],
+                    arrived_out.at[pages_of(source), kind, :, cols],
+                    z_ss.at[c, kind, step],
+                    z_rs.at[c, kind, step],
+                    {"grp": source},
+                )
     for store in stores:
         store.wait()
     for copy in pending:
         copy.wait_send()
 
 
-def front(dims, picked, inverse, meta, hidden, gain, token_keys, token_values, wq, pool, res, wo):
+def fused_step(dims, picked, inverse, *args):
+    meta, hidden, gain, token_keys, token_values, wq, pool, res, wo, mlp_gain, wg, wu, wd = args
     groups, ranks, cap, kv_here, heads = (dims[name] for name in ("groups", "ranks", "cap", "kv_here", "heads"))
     hgw = heads // ranks * HEAD_DIM
     part = heads * HEAD_DIM // ranks
@@ -741,6 +922,14 @@
     tokens = pool.shape[2]
     rows = 8 * (ranks + ranks * tiles)
     rows = -(-rows // 128) * 128
+    model = wo.shape[1]
+    cw = min(512, hidden.shape[1])
+    chunks = model // cw
+    block = slots // (2 * ranks)
+    half_rows = slots // 2
+    tile_n = 256 if wg.shape[1] % 256 == 0 else wg.shape[1]
+    ring = min(RING, wg.shape[1] // tile_n)
+    down_ring = min(DOWN_RING, chunks)
     half = lambda width: width // 2 if width >= 256 else width
     f32, bf16 = jnp.float32, jnp.bfloat16
     chunk = lambda count: [pltpu.VMEM((count, 2, tokens, HEAD_DIM), bf16) for _ in range(kv_here)]
@@ -781,7 +970,26 @@
         pltpu.VMEM((everyone, 8, 128), f32),
         pltpu.VMEM((rows, 128), f32),
         pltpu.VMEM((rows, part), f32),
+        pltpu.VMEM((ranks, 2, block, part), bf16),
+        pltpu.VMEM((chunks, half_rows, cw), f32),
+        pltpu.VMEM((chunks, half_rows, cw), bf16),
+        pltpu.VMEM((chunks, half_rows, cw), bf16),
+        pltpu.VMEM((chunks, ranks, block, cw), bf16),
+        pltpu.VMEM((chunks, ranks, block, cw), bf16),
+        pltpu.VMEM((chunks, half_rows, cw), bf16),
+        pltpu.VMEM((chunks, half_rows, cw), bf16),
+        pltpu.VMEM((chunks, ranks, block, cw), bf16),
+        pltpu.VMEM((chunks, ranks, block, cw), bf16),
+        pltpu.VMEM((chunks, block, cw), bf16),
+        pltpu.VMEM((chunks, 2, ranks, block, cw), bf16),
+        pltpu.VMEM((slots, model), bf16),
+        pltpu.VMEM((slots, wg.shape[1]), bf16),
+        pltpu.VMEM((ring, model, tile_n), bf16),
+        pltpu.VMEM((ring, model, tile_n), bf16),
+        pltpu.VMEM((down_ring, wd.shape[0], cw), bf16),
         dma(kv_here + 3),
+        dma(2, ring),
+        dma(down_ring),
         dma(everyone),
         dma(everyone),
         dma(kv_here, ranks),
@@ -804,25 +1012,39 @@
         dma(everyone),
         dma(everyone),
         dma(everyone),
-        dma(kv_here),
+        dma(kv_here, 2, groups),
+        dma(kv_here, 2, groups),
+        dma(kv_here, 2),
+        dma(chunks),
+        dma(chunks),
+        dma(chunks, ranks),
+        dma(chunks, ranks),
+        dma(chunks),
+        dma(chunks),
+        dma(chunks, ranks),
+        dma(chunks, ranks),
+        dma(chunks, ranks),
+        dma(chunks, ranks),
+        dma(chunks, ranks),
+        dma(chunks, ranks),
     ]
     vmem = pl.BlockSpec(memory_space=pltpu.VMEM)
     smem = pl.BlockSpec(memory_space=pltpu.SMEM)
     hbm = pl.BlockSpec(memory_space=pl.ANY)
     return pl.pallas_call(
-        functools.partial(front_kernel, dims),
+        functools.partial(step_kernel, dims),
         out_shape=(
-            jax.ShapeDtypeStruct((slots, wo.shape[1]), f32),
+            jax.ShapeDtypeStruct((block, model), bf16),
             jax.ShapeDtypeStruct((pages,) + pool.shape[1:], bf16),
         ),
-        in_specs=[smem, smem, vmem, vmem, vmem, vmem, vmem, hbm, hbm, hbm, hbm],
+        in_specs=[smem, smem] + [vmem] * 5 + [hbm] * 4 + [vmem] + [hbm] * 3,
         out_specs=(vmem, hbm),
         scratch_shapes=scratch,
         compiler_params=pltpu.CompilerParams(
-            collective_id=1, has_side_effects=True, vmem_limit_bytes=60 << 20
+            collective_id=1, has_side_effects=True, vmem_limit_bytes=67043328
         ),
-        name="front",
-    )(picked, inverse, meta, hidden, gain, token_keys, token_values, wq, pool, res, wo)
+        name="fused_step",
+    )(picked, inverse, *args)
 
 
 def route_tables(new_owner, new_local):
@@ -884,11 +1106,6 @@
 ):
     groups = lax.axis_size("grp")
     ranks = lax.axis_size("kv")
-    pairs = lax.axis_size("tp")
-    kv_rank = lax.axis_index("kv")
-    tp_rank = lax.axis_index("tp")
-    features = hidden_states.astype(jnp.float32)
-    slots = features.shape[0]
     heads_here = w_query.shape[1] // HEAD_DIM
     kv_here = token_kv.shape[2] // HEAD_DIM
     dims = {
@@ -911,7 +1128,7 @@
         ]
     )
     meta = jnp.pad(meta, ((0, 4), (0, 0)))
-    branch, sorted_pages = front(
+    mixed, arrived = fused_step(
         dims,
         picked,
         inverse,
@@ -924,27 +1141,11 @@
         kv_pool,
         resident_cache[0],
         w_out.reshape(-1, w_out.shape[2]),
+        mlp_gain[None],
+        w_gate,
+        w_up,
+        w_down,
     )
-    arrived = lax.all_to_all(sorted_pages, "grp", split_axis=0, concat_axis=0, tiled=True)
-    width_here = features.shape[1]
-    column = jnp.arange(ranks * width_here, dtype=jnp.int32)
-    mine = (column // width_here == kv_rank) & (tp_rank == 0)
-    branch = branch + jnp.where(mine[None, :], jnp.tile(features, (1, ranks)), 0.0)
-    row_count = slots // (ranks * pairs)
-    blocks = (ranks * pairs, row_count, ranks * width_here)
-    laid = push(branch.astype(jnp.bfloat16).reshape(blocks), ("kv", "tp"), 6)
-    kept = jnp.sum(laid.astype(jnp.float32), axis=0).astype(jnp.bfloat16)
-    resid = push(kept, ("kv", "tp"), 7, True).reshape(slots, ranks * width_here)
-    resid_f = resid.astype(jnp.float32)
-    mlp_scale = lax.rsqrt(jnp.sum(resid_f * resid_f, axis=1) / D + norm_eps)
-    normed_mlp = (resid_f * mlp_gain).astype(jnp.bfloat16)
-    gate = jnp.dot(normed_mlp, w_gate, preferred_element_type=jnp.float32) * mlp_scale[:, None]
-    upward = jnp.dot(normed_mlp, w_up, preferred_element_type=jnp.float32) * mlp_scale[:, None]
-    hidden_units = (jax.nn.silu(gate) * upward).astype(jnp.bfloat16)
-    down = jnp.dot(hidden_units, w_down, preferred_element_type=jnp.float32)
-    down = push(down.astype(jnp.bfloat16).reshape(blocks), ("kv", "tp"), 8)
-    down = jnp.sum(down.astype(jnp.float32), axis=0)
-    mixed = (kept.astype(jnp.float32) + down).astype(jnp.bfloat16)
     new_pages = jnp.take(arrived, arrived_at, axis=0, mode="clip")
     return (mixed, new_pages[None])
 

time: 194 us -> 145 us (0.75)
  matrix products: 22 us -> 0 us
  waiting for transfers between devices: 8.91 us -> 0 us
  other arithmetic: 11.6 us -> 3.89 us
  starting transfers between devices: 5.17 us -> 0 us
  Pallas kernels: 132 us -> 128 us
    dot_general x2 -> x0, matrix products: 22 us -> none  [the longest x1 14.8 us: per_device(): down = jnp.dot(hidden_units, w_down, preferred_element_type=jnp.float32)]
    all_to_all x1 -> x0, waiting for transfers between devices: 8.91 us -> none  [per_device(): lax.all_to_all(sorted_pages, 'grp', split_axis=0, concat_axis=0, tiled=True)]
    all_to_all x1 -> x0, starting transfers between devices: 5.17 us -> none  [per_device(): lax.all_to_all(sorted_pages, 'grp', split_axis=0, concat_axis=0, tiled=True)]
    reduce_sum x3 -> x0, other arithmetic: 4.94 us -> none  [the longest x1 2.06 us: per_device(): kept = jnp.sum(laid.astype(jnp.float32), axis=0).astype(jnp.bfloat16)]
    convert_element_type x3 -> x0, other arithmetic: 3.37 us -> none  [the longest x1 1.43 us: per_device(): normed_mlp = (resid_f * mlp_gain).astype(jnp.bfloat16)]
    pallas_call x4 -> x1, Pallas kernels: 132 us -> 128 us  [fused_step(): pl.pallas_call(functools.partial(step_kernel, dims), out_shape=(jax.Shape...]
  transfers between devices with their start and end apart: 1 -> 0, of which waited for: 1 -> 0; matrix products, arithmetic and copies ran while one was open for 17% -> 0% of each run, Pallas kernels for 26% -> 0%
where the time goes in v2:
time: 145 us
  Pallas kernels  128 us (88%)
  local copies, waits for them, and re-layouts  11.8 us (8%)
  other arithmetic  3.89 us (3%)
    pallas_call x1, Pallas kernels, fused_step(): pl.pallas_call(functools.partial(step_kernel, dims), out_shape=(jax.Shape...  128 us
    gather x1, local copies, waits for them, and re-layouts, per_device(): new_pages = jnp.take(arrived, arrived_at, axis=0, mode='clip')  5.17 us

profile of v2, /device:TPU:0, one launch (start us, length us, event | category | flops | bytes accessed | tf_op | source)
XLA Modules:
  0.0 144.6 jit_solution(12061975654357362975)
XLA Ops:
  0.6 0.8 reshape.312
  1.4 0.8 reshape.309
  2.2 0.1 broadcast_in_dim.100
  2.3 0.8 reshape.307
  3.1 0.1 reshape.308
  3.2 0.1 broadcast_compare_fusion
  3.2 0.2 reduce_window_sum.18
  3.5 0.1 select_reduce_fusion.3
  3.6 0.1 reshape.311
  3.7 0.1 convert_reduce_fusion
  3.8 0.1 convert_reduce_fusion.1
  3.9 0.7 select_reduce_fusion.2.inverse
  4.7 0.8 select_reduce_fusion.1
  5.5 0.7 pad_add_fusion
  6.1 0.6 pad.22.meta
  6.7 0.2 reduce_window_sum.17
  7.0 0.1 select_reduce_fusion.4
  7.1 0.6 reshape.310.picked
  7.7 0.6 pad_clamp_fusion
  8.3 1.5 %fusion.5 = (bf16[128,1,512]{2,1,0:T(2,128)(2,1)S(1)}, bf16[128,1,512]{2,1,0:T(2,128)(2,1)S(1)}) fusion(bf16[128,2,512]{2,1,0:T(2,128)(2,1)} %param.33), kind=kLoop, calls=%fused_computation.56 | loop fusion | bytes 524288 | tf_op jit(solution)/shard_map/slice | solution.py:1139
  9.8 0.7 copy_bitcast_fusion
  10.5 128.2 %fused_step.1 = (bf16[16,4096]{1,0:T(8,128)(2,1)}, bf16[16,2,128,512]{3,2,1,0:T(8,128)(2,1)}) custom-call(s32[16]{0:T(128)} %reshape.310.picked, s32[16]{0:T(128)} %select_reduce_fusion.2.inverse, s32[8,128]{1,0:T(8,128)} %pad.22.meta, bf16[128,1024]{1,0:T(8,128)(2,1)} %hidden.1, f32[1,1024]{1,0:T(1,128)} %bitcast.57, ...), custom_call_target="tpu_custom_call" | custom-call | tf_op jit(solution)/shard_map/fused_step/pallas_call | solution.py:1034
  138.8 0.0 copy-start
  138.8 5.2 %gather_fusion = bf16[16,2,128,512]{3,2,1,0:T(8,128)(2,1)} fusion(bf16[16,2,128,512]{3,2,1,0:T(8,128)(2,1)} %get-tuple-element.5, s32[1024]{0:T(1024)} %pad_clamp_fusion), kind=kCustom, calls=%fused_computation | custom fusion | bytes 8388672 | tf_op jit(solution)/shard_map/jit(_take)/gather | solution.py:1149
  144.0 0.0 copy-done
  144.0 0.7 copy.37
  (12 shorter events, 0.1 us)
Async XLA Ops:
  138.8 5.2 %copy-start = (bf16[16,4096]{1,0:T(8,128)(2,1)S(1)}, bf16[16,4096]{1,0:T(8,128)(2,1)}, u32[]{:S(2)}) copy-start(bf16[16,4096]{1,0:T(8,128)(2,1)} %get-tuple-element.21) | copy-start | bytes 393220

commit v3 on v2

v3 whole, which is shorter than its diff:
```python
import functools

import jax
import jax.numpy as jnp
from jax import lax
from jax.experimental import pallas as pl
from jax.experimental.pallas import tpu as pltpu
from jax.sharding import PartitionSpec as P

D = 4096
HEADS = 32
KV_HEADS = 8
HEAD_DIM = 128
NPR = 4


neg_fill = -1e30
norm_eps = 1e-05


RING = 4
DOWN_RING = 4


def split2(x):
    high = x.astype(jnp.bfloat16)
    return high, (x - high.astype(jnp.float32)).astype(jnp.bfloat16)


def split3(x):
    high = x.astype(jnp.bfloat16)
    rest = x - high.astype(jnp.float32)
    middle = rest.astype(jnp.bfloat16)
    return high, middle, (rest - middle.astype(jnp.float32)).astype(jnp.bfloat16)


def mm(a, b):
    return jnp.dot(a, b, preferred_element_type=jnp.float32)


def mm_nt(a, b):
    return lax.dot_general(a, b, (((1,), (1,)), ((), ())), preferred_element_type=jnp.float32)


def rows_of(shape):
    return lax.broadcasted_iota(jnp.int32, shape, 0)


def lanes_of(shape):
    return lax.broadcasted_iota(jnp.int32, shape, 1)


def half_turn(x):
    return pltpu.roll(x, 4, 0)


def fold(tile, odd):
    if tile.shape[1] < 256:
        return tile
    half = tile.shape[1] // 2
    low, high = tile[:, :half], tile[:, half:]
    top = rows_of(low.shape) < 4
    if odd:
        return jnp.where(top, half_turn(low), high)
    return jnp.where(top, low, half_turn(high))


def pick_rows(first, second, odd):
    first = jnp.where(odd, half_turn(first), first)
    second = jnp.where(odd, second, half_turn(second))
    return jnp.where(rows_of(first.shape) < 4, first, second)


def unfold(first, second, width, odd):
    if width < 256:
        return pick_rows(first, second, odd)
    top = rows_of(first.shape) < 4
    low = jnp.where(top, first, half_turn(second))
    high = jnp.where(top, half_turn(first), second)
    return jnp.concatenate([low, high], axis=1)


def column_of(row, keys, offset):
    wide = jnp.broadcast_to(row, (8, 128)).astype(jnp.float32)
    hit = jnp.broadcast_to(keys, (8, 128)) == rows_of((8, 128)) + offset
    return jnp.sum(jnp.where(hit, wide, 0.0), axis=1, keepdims=True)


def place_in_group(groups, ranks):
    grp = lax.axis_index("grp")
    kv = lax.axis_index("kv")
    me = grp * ranks + kv

    def flat(index):
        return {"grp": index // ranks, "kv": lax.rem(index, ranks)}

    return grp, kv, me, flat


def step_kernel(
    dims,
    owner,
    local,
    new_slot,
    new_len,
    kept_slot,
    kept_len,
    hidden_hbm,
    gain,
    token_hbm,
    wq_hbm,
    pool_hbm,
    res_hbm,
    wo_hbm,
    mlp_gain,
    wg_hbm,
    wu_hbm,
    wd_hbm,
    mixed_out,
    arrived_out,
    meta_out,
    table,
    owner_v,
    local_v,
    meta,
    hidden,
    token_v,
    pool_v,
    send_v,
    recv_v,
    sorted_v,
    res_v,
    wq_v,
    wo_v,
    meta_v,
    qpart,
    ss_send,
    ss_recv,
    onehot,
    onehot_t,
    near_q_send,
    near_q_recv,
    rows_send,
    rows_recv,
    far_q_send,
    far_q_recv,
    own_t,
    own_send,
    own_recv,
    near_send,
    near_recv,
    far_send,
    far_recv,
    all_lse,
    all_acc,
    piece_v,
    branch_v,
    feature_v,
    keep_v,
    r1_send,
    r1_recv,
    r2_send,
    r2_recv,
    d1_send,
    d1_recv,
    d2_send,
    d2_recv,
    kept_v,
    resid_v,
    gate_v,
    up_v,
    units_v,
    wg_v,
    wu_v,
    wd_v,
    load_sem,
    gate_sem,
    down_sem,
    meta_ss,
    meta_rs,
    page_ss,
    page_rs,
    q_ss,
    q_rs,
    s_ss,
    s_rs,
    nq_ss,
    nq_rs,
    fq_ss,
    fq_rs,
    own_ss,
    own_rs,
    na_ss,
    na_rs,
    fa_ss,
    fa_rs,
    z_ss,
    z_rs,
    z_own,
    r1_ss,
    r1_rs,
    r2_ss,
    r2_rs,
    d1_ss,
    d1_rs,
    d2_ss,
    d2_rs,
    g_ss,
    g_rs,
    gp_ss,
    gp_rs,
):
    groups, ranks, cap, kv_here, heads = (dims[name] for name in ("groups", "ranks", "cap", "kv_here", "heads"))
    ratio = heads // kv_here
    hg = heads // ranks
    hgw = hg * HEAD_DIM
    span = HEAD_DIM // ranks
    part = heads * span
    per_tile = HEAD_DIM // span
    everyone = groups * ranks
    tiles = groups * NPR // 8
    count_tiles = ranks + ranks * tiles
    grp, kv, me, flat = place_in_group(groups, ranks)
    tp = lax.axis_index("tp")
    partner = {"tp": 1 - tp}
    odd_here = lax.rem(grp, 2) == 1
    slots = hidden.shape[0]

    def kv_peer(step):
        return lax.rem(kv + step, ranks)

    def kv_from(step):
        return lax.rem(kv - step + ranks, ranks)

    def all_peer(step):
        return lax.rem(me + step, everyone)

    def all_from(step):
        return lax.rem(me - step + everyone, everyone)

    pending = []

    def remote(src, dst, ss, rs, where):
        copy = pltpu.make_async_remote_copy(
            src_ref=src,
            dst_ref=dst,
            send_sem=ss,
            recv_sem=rs,
            device_id=where,
            device_id_type=pl.DeviceIdType.MESH,
        )
        copy.start()
        pending.append(copy)

    def arrive(src, dst, ss, rs, where):
        pltpu.make_async_remote_copy(
            src_ref=src,
            dst_ref=dst,
            send_sem=ss,
            recv_sem=rs,
            device_id=where,
            device_id_type=pl.DeviceIdType.MESH,
        ).wait_recv()

    loads = []
    for c in range(kv_here):
        cols = pl.ds(c * HEAD_DIM, HEAD_DIM)
        loads.append(
            pltpu.make_async_copy(pool_hbm.at[:, :, :, cols], pool_v[c], load_sem.at[c])
        )
    load_q = pltpu.make_async_copy(wq_hbm, wq_v, load_sem.at[kv_here])
    load_r = pltpu.make_async_copy(res_hbm, res_v, load_sem.at[kv_here + 1])
    load_o = pltpu.make_async_copy(wo_hbm, wo_v, load_sem.at[kv_here + 2])
    load_h = pltpu.make_async_copy(hidden_hbm, hidden, load_sem.at[kv_here + 3])
    load_t = pltpu.make_async_copy(token_hbm, token_v, load_sem.at[kv_here + 4])
    loads[0].start()
    load_h.start()
    load_q.start()
    for copy in loads[1:]:
        copy.start()
    load_r.start()
    load_t.start()
    load_o.start()

    barrier = pltpu.get_barrier_semaphore()
    for step in range(1, everyone):
        pl.semaphore_signal(
            barrier, inc=1, device_id=flat(all_peer(step)), device_id_type=pl.DeviceIdType.MESH
        )
    pl.semaphore_signal(
        barrier, inc=1, device_id=partner, device_id_type=pl.DeviceIdType.MESH
    )
    per = owner.shape[1] // ranks
    wide = owner_v.shape[1]
    owner_v[...] = jnp.full((8, wide), -1, jnp.int32)
    local_v[...] = jnp.zeros((8, wide), jnp.int32)
    owner_v[: owner.shape[0], : owner.shape[1]] = owner[...]
    local_v[: owner.shape[0], : owner.shape[1]] = local[...]
    owners, locals_ = owner_v[...], local_v[...]
    table_row, table_lane = rows_of((8, wide)), lanes_of((8, wide))
    place = lax.rem(table_lane, per)
    column = table_lane // per

    def before(match):
        count = match.astype(jnp.int32)
        ahead, behind = count, count
        shift = 1
        while shift < per:
            ahead = ahead + jnp.where(place >= shift, pltpu.roll(ahead, shift, 1), 0)
            behind = behind + jnp.where(
                place < per - shift, pltpu.roll(behind, wide - shift, 1), 0
            )
            shift *= 2
        return ahead - count, ahead - count + behind

    def order(match):
        ahead, whole = before(match)
        for shift in range(1, groups):
            ahead = ahead + jnp.where(table_row >= shift, pltpu.roll(whole, shift, 0), 0)
        return ahead

    def total_of(values):
        return jnp.sum(jnp.sum(values, axis=0, keepdims=True))

    mine = owners == me
    mine_order = order(mine)
    for k in range(ranks):
        for a in range(cap):
            hit = mine & (mine_order == a) & (column == k)
            table[k * cap + a] = total_of(jnp.where(hit, locals_, 0))
    row_base = grp * ranks
    here = (owners >= row_base) & (owners < row_base + ranks) & (column == kv)
    here_order = order(here)
    landed = jnp.zeros((8, wide), jnp.int32)
    for k in range(ranks):
        match = here & (owners == row_base + k)
        landed = landed + jnp.where(match, k * cap + order(match), 0)
    for i in range(groups * NPR):
        hit = here & (here_order == i)
        table[ranks * cap + i] = total_of(jnp.where(hit, landed, 0))
    spot = jnp.zeros((8, wide), jnp.int32)
    for g in range(groups):
        match = (owners >= g * ranks) & (owners < (g + 1) * ranks)
        spot = spot + jnp.where(match, g * NPR + before(match)[0], 0)
    spot = jnp.where((table_row == grp) & (column == kv), spot, 0)
    spot = jnp.broadcast_to(jnp.sum(spot, axis=0, keepdims=True), (8, wide))
    spot = pltpu.roll(spot, lax.rem(wide - kv * per, wide), 1)[:1, :128]
    meta[...] = jnp.zeros((8, 128), jnp.int32)
    meta[0:1, :per] = new_slot[...]
    meta[1:2, :per] = new_len[...]
    meta[2:3, : kept_slot.shape[1]] = kept_slot[...]
    meta[3:4, : kept_slot.shape[1]] = kept_len[...]
    meta[4:5, :] = jnp.where(lanes_of((1, 128)) < per, spot, -1)
    meta[5:6, :] = lanes_of((1, 128))
    meta_out[...] = meta[...]
    pl.semaphore_wait(barrier, everyone)

    for step in range(1, everyone):
        remote(meta, meta_v.at[me], meta_ss.at[step], meta_rs.at[step], flat(all_peer(step)))
    meta_v[me] = meta[...]

    loaded = set()

    def send_pages(c, kind):
        if c not in loaded:
            loads[c].wait()
            loaded.add(c)

        def pick(i, carry):
            for a in range(cap):
                target = lax.rem(kv + i, ranks) * cap + a
                send_v[c][kind, i * cap + a] = pool_v[c][table[target], kind]
            return carry

        for a in range(cap):
            recv_v[2 * c + kind][kv * cap + a] = pool_v[c][table[kv * cap + a], kind]
        lax.fori_loop(1, ranks, pick, 0)
        for step in range(1, ranks):
            remote(
                send_v[c].at[kind, pl.ds(step * cap, cap)],
                recv_v[2 * c + kind].at[pl.ds(kv * cap, cap)],
                page_ss.at[c, kind, step],
                page_rs.at[c, kind, step],
                {"kv": kv_peer(step)},
            )

    def sort_pages(c, kind):
        for step in range(1, ranks):
            source = kv_from(step)
            arrive(
                send_v[c].at[kind, pl.ds(step * cap, cap)],
                recv_v[2 * c + kind].at[pl.ds(source * cap, cap)],
                page_ss.at[c, kind, step],
                page_rs.at[c, kind, step],
                {"kv": source},
            )

        def sort(i, carry):
            sorted_v[c][kind, i] = recv_v[2 * c + kind][table[ranks * cap + i]]
            return carry

        lax.fori_loop(0, groups * NPR, sort, 0)

    def pages_of(group):
        return pl.ds(pl.multiple_of(group * NPR, NPR), NPR)

    def grp_peer(step):
        return lax.rem(grp + step, groups)

    def grp_from(step):
        return lax.rem(grp - step + groups, groups)

    stores = []

    every_step = tuple(range(1, groups))

    def forward_pages(c, kind, steps=every_step, own=True):
        cols = pl.ds(c * HEAD_DIM, HEAD_DIM)
        for step in steps:
            peer = grp_peer(step)
            remote(
                sorted_v[c].at[kind, pages_of(peer)],
                arrived_out.at[pages_of(grp), kind, :, cols],
                z_ss.at[c, kind, step],
                z_rs.at[c, kind, step],
                {"grp": peer},
            )
        if not own:
            return
        store = pltpu.make_async_copy(
            sorted_v[c].at[kind, pages_of(grp)],
            arrived_out.at[pages_of(grp), kind, :, cols],
            z_own.at[c, kind],
        )
        store.start()
        stores.append(store)

    send_pages(0, 0)
    send_pages(0, 1)

    load_h.wait()
    load_q.wait()
    features = hidden[...].astype(jnp.float32)
    normed = (features * gain[...]).astype(jnp.bfloat16)
    for j in range(ranks):
        qpart[j] = mm(normed, wq_v[:, j * hgw : (j + 1) * hgw])
    ring, cw = wg_v.shape[0], wg_v.shape[1]
    chunks = wd_hbm.shape[1] // cw
    down_ring = wd_v.shape[0]

    def gate_loads(n):
        rows = pl.ds(n * cw, cw)
        slot = n % ring
        return (
            pltpu.make_async_copy(wg_hbm.at[rows], wg_v.at[slot], gate_sem.at[0, slot]),
            pltpu.make_async_copy(wu_hbm.at[rows], wu_v.at[slot], gate_sem.at[1, slot]),
        )

    def down_load(c):
        slot = c % down_ring
        return pltpu.make_async_copy(
            wd_hbm.at[:, pl.ds(c * cw, cw)], wd_v.at[slot], down_sem.at[slot]
        )

    for n in range(ring):
        for copy in gate_loads(n):
            copy.start()
    for c in range(down_ring):
        down_load(c).start()
    squares = jnp.sum(features * features, axis=1, keepdims=True)
    ss_send[...] = jnp.transpose(jnp.broadcast_to(squares, (slots, 128)))[:8]
    ss_recv[kv] = ss_send[...]
    for step in range(1, ranks):
        peer = kv_peer(step)
        remote(ss_send, ss_recv.at[kv], s_ss.at[step], s_rs.at[step], {"kv": peer})
    load_t.wait()
    own_keys = token_v[...].astype(jnp.float32)[:, 0]
    slot_lane = lanes_of((slots, 128))
    own = jnp.zeros((slots, 128), jnp.float32)
    for head in range(heads):
        at = (head % hg) * HEAD_DIM
        key = own_keys[:, (head // ratio) * HEAD_DIM : (head // ratio + 1) * HEAD_DIM]
        score = jnp.sum(qpart[head // hg, :, at : at + HEAD_DIM] * key, axis=1, keepdims=True)
        own = jnp.where(slot_lane == head, score, own)
    own_send[...] = jnp.transpose(own)[:heads]
    own_recv[kv] = own_send[...]

    for step in range(1, everyone):
        source = all_from(step)
        arrive(meta, meta_v.at[source], meta_ss.at[step], meta_rs.at[step], flat(source))
    slot_rows = []
    for k in range(ranks):
        facts = meta_v[grp * ranks + k]
        slot_rows.append(column_of(facts[2:3], facts[5:6], 0))
    for k in range(ranks):
        facts = meta_v[grp * ranks + k]
        for t in range(tiles):
            slot_rows.append(column_of(facts[0:1], facts[4:5], 8 * t))
    for i, column in enumerate(slot_rows):
        onehot[8 * i : 8 * i + 8, :] = (
            column == lanes_of((8, slots)).astype(jnp.float32)
        ).astype(jnp.float32)
    for i in range(8 * count_tiles, onehot.shape[0], 8):
        onehot[i : i + 8, :] = jnp.zeros((8, slots), jnp.float32)

    hot = onehot[...].astype(jnp.bfloat16)

    def spread_rows(value):
        high, middle, low = split3(value)
        return mm(hot, high) + mm(hot, middle) + mm(hot, low)

    far_rows = 8 * ranks * tiles
    for j in range(ranks):
        chosen = spread_rows(qpart[j])
        for k in range(ranks):
            near_q_send[k, :, j * hgw : (j + 1) * hgw] = chosen[8 * k : 8 * k + 8]
        rows_send[j] = chosen[8 * ranks : 8 * ranks + far_rows]
    for step in range(1, ranks):
        peer = kv_peer(step)
        remote(rows_send.at[peer], rows_recv.at[kv], q_ss.at[step], q_rs.at[step], {"kv": peer})
        remote(
            near_q_send.at[peer], near_q_recv.at[kv], nq_ss.at[step], nq_rs.at[step], {"kv": peer}
        )
        remote(own_send, own_recv.at[kv], own_ss.at[step], own_rs.at[step], {"kv": peer})
    send_pages(1, 0)
    send_pages(1, 1)
    sort_pages(0, 0)
    forward_pages(0, 0)
    sort_pages(0, 1)
    forward_pages(0, 1)

    for step in range(1, ranks):
        source = kv_from(step)
        arrive(ss_send, ss_recv.at[source], s_ss.at[step], s_rs.at[step], {"kv": source})
        arrive(
            rows_send.at[source], rows_recv.at[source], q_ss.at[step], q_rs.at[step], {"kv": source}
        )
    total_ss = ss_recv[0]
    for j in range(1, ranks):
        total_ss = total_ss + ss_recv[j]
    row_scale = lax.rsqrt(total_ss[0:1] / D + norm_eps) * HEAD_DIM ** (-0.5)
    page_scale = spread_rows(jnp.transpose(jnp.broadcast_to(row_scale, (128, slots))))
    far_scale = page_scale[8 * ranks : 8 * ranks + far_rows]
    chosen = []
    for i in range(hg):
        cols = slice(i * HEAD_DIM, (i + 1) * HEAD_DIM)
        total = rows_send[kv, :, cols]
        for step in range(1, ranks):
            total = total + rows_recv[kv_from(step), :, cols]
        chosen.append(total * far_scale)
    chosen = jnp.concatenate(chosen, axis=1)
    for k in range(ranks):
        for t in range(tiles):
            at = 8 * (k * tiles + t)
            tile = chosen[at : at + 8]
            far_q_send[(2 * t) * ranks + k] = fold(tile, False)
            far_q_send[(2 * t + 1) * ranks + k] = fold(tile, True)
    far_q_recv[me] = far_q_send[me]
    for step in range(1, everyone):
        peer = all_peer(step)
        remote(
            far_q_send.at[peer], far_q_recv.at[me], fq_ss.at[step], fq_rs.at[step], flat(peer)
        )

    send_pages(2, 0)
    sort_pages(1, 0)
    forward_pages(1, 0)

    row_id = rows_of((8, 128))
    row_masks = [
        jnp.concatenate([(row_id == p).astype(jnp.bfloat16)] * ratio, axis=0) for p in range(8)
    ]

    def page_tile(queries, keys, values, lengths):
        q_high, q_middle, q_low = split3(jnp.concatenate(queries, axis=0))
        rows = 8 * ratio
        scores = jnp.zeros((3 * rows, HEAD_DIM), jnp.float32)
        for p in range(8):
            mask = row_masks[p]
            stacked = jnp.concatenate([q_high * mask, q_middle * mask, q_low * mask], axis=0)
            scores = scores + mm_nt(stacked, keys(p))
        scores = scores[:rows] + scores[rows : 2 * rows] + scores[2 * rows :]
        usable = lanes_of((rows, 128)).astype(jnp.float32) < jnp.concatenate(
            [lengths] * ratio, axis=0
        )
        scores = jnp.where(usable, scores, neg_fill)
        top = jnp.max(scores, axis=1, keepdims=True)
        weights = jnp.where(usable, jnp.exp(scores - top), 0.0)
        total = jnp.sum(weights, axis=1, keepdims=True)
        w_high, w_low = split2(weights)
        acc = jnp.zeros((2 * rows, HEAD_DIM), jnp.float32)
        for p in range(8):
            mask = row_masks[p]
            stacked = jnp.concatenate([w_high * mask, w_low * mask], axis=0)
            acc = acc + mm(stacked, values(p))
        acc = (acc[:rows] + acc[rows:]) / total
        return acc, top + jnp.log(total)

    lane_id = lanes_of((8, 128))

    lane_part = lane_id // span
    chunk_lanes = ratio * span

    def pack_acc(acc, k):
        merged = None
        for i in range(ratio):
            turn = (span * (i - k)) % HEAD_DIM
            moved = acc[8 * i : 8 * i + 8]
            if turn:
                moved = pltpu.roll(moved, turn, 1)
            merged = moved if merged is None else jnp.where(lane_part == i, moved, merged)
        return merged

    def pack_lse(lse):
        merged = jnp.zeros((8, 128), jnp.float32)
        for i in range(ratio):
            merged = jnp.where(lane_part == i, lse[8 * i : 8 * i + 8], merged)
        return merged

    for step in range(1, ranks):
        source = kv_from(step)
        arrive(
            near_q_send.at[source],
            near_q_recv.at[source],
            nq_ss.at[step],
            nq_rs.at[step],
            {"kv": source},
        )
    load_r.wait()
    near_scale = jnp.zeros((8, 128), jnp.float32)
    for k in range(ranks):
        near_scale = jnp.where(kv == k, page_scale[8 * k : 8 * k + 8], near_scale)
    near_length = column_of(meta[3:4], meta[5:6], 0)
    for j in range(kv_here):
        queries = []
        for i in range(ratio):
            head = j * ratio + i
            cols = slice(head * HEAD_DIM, (head + 1) * HEAD_DIM)
            total = near_q_send[kv, :, cols]
            for step in range(1, ranks):
                total = total + near_q_recv[kv_from(step), :, cols]
            queries.append(total * near_scale)
        cols = slice(j * HEAD_DIM, (j + 1) * HEAD_DIM)
        acc, lse = page_tile(
            queries,
            lambda p: res_v[p, 0, :, cols],
            lambda p: res_v[p, 1, :, cols],
            near_length,
        )
        near_lse = pack_lse(lse)
        for k in range(ranks):
            near_send[k, j, :8] = pack_acc(acc, k)
            near_send[k, j, 8:] = near_lse
    near_recv[kv] = near_send[kv]
    for step in range(1, ranks):
        peer = kv_peer(step)
        remote(near_send.at[peer], near_recv.at[kv], na_ss.at[step], na_rs.at[step], {"kv": peer})
    send_pages(2, 1)
    send_pages(3, 0)
    send_pages(3, 1)

    for step in range(1, everyone):
        source = all_from(step)
        arrive(
            far_q_send.at[source],
            far_q_recv.at[source],
            fq_ss.at[step],
            fq_rs.at[step],
            flat(source),
        )
    far_lengths = []
    for t in range(tiles):
        offset = grp * NPR
        one, two = meta_v[(2 * t) * ranks + kv], meta_v[(2 * t + 1) * ranks + kv]
        first = column_of(one[1:2], one[4:5], offset)
        second = column_of(two[1:2], two[4:5], offset - 4)
        far_lengths.append(jnp.where(rows_of((8, 1)) < 4, first, second))
    upper = rows_of((8, 128)) < 4

    def far_attention(c):
        for t in range(tiles):
            queries = []
            for i in range(ratio):
                head = c * ratio + i
                k = head // hg
                wide_q = unfold(
                    far_q_recv[(2 * t) * ranks + k],
                    far_q_recv[(2 * t + 1) * ranks + k],
                    hgw,
                    odd_here,
                )
                at = (head % hg) * HEAD_DIM
                queries.append(wide_q[:, at : at + HEAD_DIM])
            acc, lse = page_tile(
                queries,
                lambda p: sorted_v[c][0, 8 * t + p],
                lambda p: sorted_v[c][1, 8 * t + p],
                far_lengths[t],
            )
            lse = pack_lse(lse)
            for k in range(ranks):
                tile = pack_acc(acc, k)
                far_send[c, (2 * t) * ranks + k] = jnp.where(upper, tile, half_turn(lse))
                far_send[c, (2 * t + 1) * ranks + k] = jnp.where(upper, half_turn(tile), lse)
        far_recv[c, me] = far_send[c, me]
        for step in range(1, everyone):
            peer = all_peer(step)
            remote(
                far_send.at[c, peer],
                far_recv.at[c, me],
                fa_ss.at[c, step],
                fa_rs.at[c, step],
                flat(peer),
            )

    choose = (
        rows_of((HEAD_DIM, 128)) == kv * span + lax.rem(lanes_of((HEAD_DIM, 128)), span)
    ).astype(jnp.bfloat16)
    used = 8 * count_tiles
    diagonal = (row_id == lax.rem(lane_id, 8)).astype(jnp.float32)
    slot_id = rows_of((slots, 128)).astype(jnp.float32)
    wide_lane = lanes_of((slots, 128))
    slot_lanes = [jnp.sum(column * diagonal, axis=0, keepdims=True) for column in slot_rows]

    def wait_far(c):
        for step in range(1, everyone):
            source = all_from(step)
            arrive(
                far_send.at[c, source],
                far_recv.at[c, source],
                fa_ss.at[c, step],
                fa_rs.at[c, step],
                flat(source),
            )

    def combine(c):
        for k in range(ranks):
            all_acc[8 * k : 8 * k + 8, :] = near_recv[k, c, :8]
            all_lse[8 * k : 8 * k + 8, :] = near_recv[k, c, 8:]
            for t in range(tiles):
                at = 8 * (ranks + k * tiles + t)
                one, two = far_recv[c, (2 * t) * ranks + k], far_recv[c, (2 * t + 1) * ranks + k]
                all_acc[at : at + 8, :] = jnp.where(upper, one, half_turn(two))
                all_lse[at : at + 8, :] = jnp.where(upper, half_turn(one), two)
        top = jnp.full((slots, 128), neg_fill, jnp.float32)
        for i, owner_lane in enumerate(slot_lanes):
            value = jnp.sum(all_lse[8 * i : 8 * i + 8, :] * diagonal, axis=0, keepdims=True)
            top = jnp.maximum(top, jnp.where(slot_id == owner_lane, value, neg_fill))
        for shift in (1, 2, 4):
            up = pltpu.roll(top, shift, 1)
            down = pltpu.roll(top, 128 - shift, 1)
            top = jnp.maximum(top, jnp.where((wide_lane & shift) != 0, up, down))
        widen = (
            rows_of((128, 128)) == c * ratio + lanes_of((128, 128)) // span
        ).astype(jnp.bfloat16)
        high, middle, low = split3(own_all)
        own_score = mm(high, widen) + mm(middle, widen) + mm(low, widen)
        top = jnp.maximum(top, own_score)
        high, middle, low = split3(top)
        page_top = mm(hot, high) + mm(hot, middle) + mm(hot, low)
        page_weight = jnp.exp(all_lse[...] - page_top)
        own_weight = jnp.exp(own_score - top)
        hot_t = onehot_t[...]
        high, low = split2(page_weight)
        total = mm(hot_t, high) + mm(hot_t, low) + own_weight
        high, low = split2(all_acc[...] * page_weight)
        gathered = mm(hot_t, high) + mm(hot_t, low)
        values = token_v[:, :, c * HEAD_DIM : (c + 1) * HEAD_DIM].astype(jnp.float32)[:, 1]
        own_piece = mm(values.astype(jnp.bfloat16), choose)
        return (gathered + own_weight * own_piece) / total

    far_attention(0)
    sort_pages(1, 1)
    far_attention(1)
    forward_pages(1, 1)
    sort_pages(2, 0)
    sort_pages(2, 1)
    far_attention(2)
    middle = groups // 2
    forward_pages(2, 0, (middle,), False)
    onehot_t[...] = jnp.transpose(onehot[...]).astype(jnp.bfloat16)
    for at in range(used, all_lse.shape[0], 8):
        all_lse[at : at + 8, :] = jnp.zeros((8, 128), jnp.float32)
        all_acc[at : at + 8, :] = jnp.zeros((8, 128), jnp.float32)
    for step in range(1, ranks):
        source = kv_from(step)
        arrive(own_send, own_recv.at[source], own_ss.at[step], own_rs.at[step], {"kv": source})
        arrive(
            near_send.at[source],
            near_recv.at[source],
            na_ss.at[step],
            na_rs.at[step],
            {"kv": source},
        )
    own_t[...] = jnp.zeros((128, slots), jnp.float32)
    own_sum = own_recv[0]
    for k in range(1, ranks):
        own_sum = own_sum + own_recv[k]
    own_t[:heads, :] = own_sum * row_scale
    own_all = jnp.transpose(own_t[...])
    rows16 = piece_v.shape[2]
    half = ranks * rows16
    for i in range(feature_v.shape[0]):
        mine = hidden[:, i * cw : (i + 1) * cw].reshape(ranks, 2, rows16, cw)
        mine = jnp.where(tp == 0, mine[:, 0], mine[:, 1]).reshape(half, cw)
        feature_v[i] = mine.astype(jnp.float32)
    sort_pages(3, 0)
    sort_pages(3, 1)
    far_attention(3)
    forward_pages(2, 0, tuple(step for step in every_step if step != middle))
    forward_pages(2, 1)
    forward_pages(3, 0)
    forward_pages(3, 1)
    fits = 128 // chunk_lanes
    for c in range(kv_here):
        wait_far(c)
        turned = combine(c)
        if fits > 1:
            turned = pltpu.roll(turned, (c * chunk_lanes) % 128, 1)
        if c % fits == 0:
            merged = turned
        else:
            merged = jnp.where(wide_lane // chunk_lanes == c % fits, turned, merged)
        if c % fits == fits - 1:
            last = c // fits
            piece_v[:, :, :, last * 128 : (last + 1) * 128] = merged.astype(jnp.bfloat16).reshape(
                ranks, 2, rows16, 128
            )
            ordered = jnp.concatenate(
                [
                    piece_v[:, side, :, last * 128 : (last + 1) * 128].reshape(half, 128)
                    for side in (1 - tp, tp)
                ],
                axis=0,
            )
            if c == 0 or fits > 1:
                load_o.wait()
            if c < kv_here - 1:
                for d in range(chunks):
                    value = mm(
                        ordered, wo_v[last * 128 : (last + 1) * 128, d * cw : (d + 1) * cw]
                    )
                    branch_v[d] = value if last == 0 else branch_v[d] + value

    def scatter_start(c, value, send, recv, ss, rs):
        send[c] = value[:half].astype(jnp.bfloat16)
        remote(send.at[c], recv.at[c], ss.at[c], rs.at[c], partner)
        keep_v[c] = value[half:]

    def scatter_middle(c, extra, first, second, sems1, sems2):
        arrive(first[0].at[c], first[1].at[c], sems1[0].at[c], sems1[1].at[c], partner)
        both = keep_v[c] + first[1][c].astype(jnp.float32)
        if extra is not None:
            both = both + extra
        second[0][c] = both.astype(jnp.bfloat16).reshape(ranks, rows16, cw)
        second[1][c, kv] = second[0][c, kv]
        for step in range(1, ranks):
            peer = kv_peer(step)
            remote(
                second[0].at[c, peer],
                second[1].at[c, kv],
                sems2[0].at[c, step],
                sems2[1].at[c, step],
                {"kv": peer},
            )

    def scatter_end(c, second, sems2):
        for step in range(1, ranks):
            source = kv_from(step)
            arrive(
                second[0].at[c, source],
                second[1].at[c, source],
                sems2[0].at[c, step],
                sems2[1].at[c, step],
                {"kv": source},
            )
        total = second[1][c, 0].astype(jnp.float32)
        for j in range(1, ranks):
            total = total + second[1][c, j].astype(jnp.float32)
        return total

    width_here = hidden.shape[1]
    lag = 2
    for c in range(chunks + lag):
        if c < chunks:
            value = mm(ordered, wo_v[last * 128 : (last + 1) * 128, c * cw : (c + 1) * cw])
            if last > 0:
                value = value + branch_v[c]
            scatter_start(c, value, r1_send, r1_recv, r1_ss, r1_rs)
        if c >= lag:
            d = c - lag
            mine = feature_v[d % feature_v.shape[0]]
            mine = jnp.where(kv == (d * cw) // width_here, mine, 0.0)
            scatter_middle(
                d, mine, (r1_send, r1_recv), (r2_send, r2_recv), (r1_ss, r1_rs), (r2_ss, r2_rs)
            )
    for c in range(chunks):
        block = scatter_end(c, (r2_send, r2_recv), (r2_ss, r2_rs)).astype(jnp.bfloat16)
        kept_v[c] = block
        resid_v[c, 1, kv] = block
        for step in range(1, ranks):
            remote(
                kept_v.at[c],
                resid_v.at[c, 1, kv],
                g_ss.at[c, step],
                g_rs.at[c, step],
                {"kv": kv_peer(step)},
            )
        remote(kept_v.at[c], resid_v.at[c, 0, kv], gp_ss.at[c, 0], gp_rs.at[c, 0], partner)
    square_sum = jnp.zeros((2 * half, 1), jnp.float32)
    for c in range(chunks + 1):
        if c < chunks:
            for step in range(1, ranks):
                source = kv_from(step)
                arrive(
                    kept_v.at[c],
                    resid_v.at[c, 1, source],
                    g_ss.at[c, step],
                    g_rs.at[c, step],
                    {"kv": source},
                )
                remote(
                    resid_v.at[c, 1, source],
                    resid_v.at[c, 0, source],
                    gp_ss.at[c, step],
                    gp_rs.at[c, step],
                    partner,
                )
        if c >= 1:
            d = c - 1
            for step in range(ranks):
                source = kv_from(step)
                arrive(
                    kept_v.at[d],
                    resid_v.at[d, 0, source],
                    gp_ss.at[d, step],
                    gp_rs.at[d, step],
                    partner,
                )
            block = resid_v[d].reshape(2 * half, cw).astype(jnp.float32)
            square_sum = square_sum + jnp.sum(block * block, axis=1, keepdims=True)
            normed = (block * mlp_gain[:, d * cw : (d + 1) * cw]).astype(jnp.bfloat16)
            slot = d % ring
            for copy in gate_loads(d):
                copy.wait()
            if d == 0:
                gate_v[...] = mm(normed, wg_v[slot])
                up_v[...] = mm(normed, wu_v[slot])
            else:
                gate_v[...] += mm(normed, wg_v[slot])
                up_v[...] += mm(normed, wu_v[slot])
            if d + ring < chunks:
                for copy in gate_loads(d + ring):
                    copy.start()
    mlp_scale = lax.rsqrt(square_sum / D + norm_eps)
    gate = gate_v[...] * mlp_scale
    units_v[...] = (gate / (1.0 + jnp.exp(-gate)) * (up_v[...] * mlp_scale)).astype(jnp.bfloat16)
    for c in range(chunks + lag):
        if c < chunks:
            down_load(c).wait()
            value = mm(units_v[...], wd_v[c % down_ring])
            scatter_start(c, value, d1_send, d1_recv, d1_ss, d1_rs)
            if c + down_ring < chunks:
                down_load(c + down_ring).start()
        if c >= lag:
            scatter_middle(
                c - lag,
                None,
                (d1_send, d1_recv),
                (d2_send, d2_recv),
                (d1_ss, d1_rs),
                (d2_ss, d2_rs),
            )
    for c in range(chunks):
        total = scatter_end(c, (d2_send, d2_recv), (d2_ss, d2_rs))
        total = total + kept_v[c].astype(jnp.float32)
        mixed_out[:, c * cw : (c + 1) * cw] = total.astype(jnp.bfloat16)
    for c in range(kv_here):
        cols = pl.ds(c * HEAD_DIM, HEAD_DIM)
        for kind in range(2):
            for step in range(1, groups):
                source = grp_from(step)
                arrive(
                    sorted_v[c].at[kind, pages_of(source)],
                    arrived_out.at[pages_of(source), kind, :, cols],
                    z_ss.at[c, kind, step],
                    z_rs.at[c, kind, step],
                    {"grp": source},
                )
    for store in stores:
        store.wait()
    for copy in pending:
        copy.wait_send()


def fused_step(dims, *args):
    owner, hidden, token_kv, wq, pool, res, wo = (args[i] for i in (0, 6, 8, 9, 10, 11, 12))
    wg, wu, wd = args[14:]
    groups, ranks, cap, kv_here, heads = (dims[name] for name in ("groups", "ranks", "cap", "kv_here", "heads"))
    hgw = heads // ranks * HEAD_DIM
    part = heads * HEAD_DIM // ranks
    everyone = groups * ranks
    pages = groups * NPR
    tiles = pages // 8
    slots = hidden.shape[0]
    tokens = pool.shape[2]
    rows = 8 * (ranks + ranks * tiles)
    rows = -(-rows // 128) * 128
    model = wo.shape[1]
    cw = min(512, hidden.shape[1])
    chunks = model // cw
    block = slots // (2 * ranks)
    half_rows = slots // 2
    ring = min(RING, chunks)
    down_ring = min(DOWN_RING, chunks)
    wide = -(-owner.shape[1] // 128) * 128
    half = lambda width: width // 2 if width >= 256 else width
    f32, bf16 = jnp.float32, jnp.bfloat16
    whole = lambda count: pltpu.VMEM((count, 2, tokens, HEAD_DIM), bf16)
    pair = lambda count: pltpu.VMEM((2, count, tokens, HEAD_DIM), bf16)
    single = lambda count: pltpu.VMEM((count, tokens, HEAD_DIM), bf16)
    dma = lambda *shape: pltpu.SemaphoreType.DMA(shape)
    scratch = [
        pltpu.SMEM((2 * pages,), jnp.int32),
        pltpu.VMEM((8, wide), jnp.int32),
        pltpu.VMEM((8, wide), jnp.int32),
        pltpu.VMEM((8, 128), jnp.int32),
        pltpu.VMEM(hidden.shape, bf16),
        pltpu.VMEM(token_kv.shape, bf16),
        [whole(pool.shape[0]) for _ in range(kv_here)],
        [pair(pages) for _ in range(kv_here)],
        [single(pages) for _ in range(2 * kv_here)],
        [pair(pages) for _ in range(kv_here)],
        pltpu.VMEM(res.shape, bf16),
        pltpu.VMEM(wq.shape, bf16),
        pltpu.VMEM(wo.shape, bf16),
        pltpu.VMEM((everyone, 8, 128), jnp.int32),
        pltpu.VMEM((ranks, slots, hgw), f32),
        pltpu.VMEM((8, slots), f32),
        pltpu.VMEM((ranks, 8, slots), f32),
        pltpu.VMEM((rows, slots), f32),
        pltpu.VMEM((slots, rows), bf16),
        pltpu.VMEM((ranks, 8, heads * HEAD_DIM), f32),
        pltpu.VMEM((ranks, 8, heads * HEAD_DIM), f32),
        pltpu.VMEM((ranks, 8 * ranks * tiles, hgw), f32),
        pltpu.VMEM((ranks, 8 * ranks * tiles, hgw), f32),
        pltpu.VMEM((everyone, 8, half(hgw)), f32),
        pltpu.VMEM((everyone, 8, half(hgw)), f32),
        pltpu.VMEM((128, slots), f32),
        pltpu.VMEM((heads, slots), f32),
        pltpu.VMEM((ranks, heads, slots), f32),
        pltpu.VMEM((ranks, kv_here, 16, 128), f32),
        pltpu.VMEM((ranks, kv_here, 16, 128), f32),
        pltpu.VMEM((kv_here, everyone, 8, 128), f32),
        pltpu.VMEM((kv_here, everyone, 8, 128), f32),
        pltpu.VMEM((rows, 128), f32),
        pltpu.VMEM((rows, 128), f32),
        pltpu.VMEM((ranks, 2, block, part), bf16),
        pltpu.VMEM((chunks, slots, cw), f32),
        pltpu.VMEM((hidden.shape[1] // cw, half_rows, cw), f32),
        pltpu.VMEM((chunks, half_rows, cw), f32),
        pltpu.VMEM((chunks, half_rows, cw), bf16),
        pltpu.VMEM((chunks, half_rows, cw), bf16),
        pltpu.VMEM((chunks, ranks, block, cw), bf16),
        pltpu.VMEM((chunks, ranks, block, cw), bf16),
        pltpu.VMEM((chunks, half_rows, cw), bf16),
        pltpu.VMEM((chunks, half_rows, cw), bf16),
        pltpu.VMEM((chunks, ranks, block, cw), bf16),
        pltpu.VMEM((chunks, ranks, block, cw), bf16),
        pltpu.VMEM((chunks, block, cw), bf16),
        pltpu.VMEM((chunks, 2, ranks, block, cw), bf16),
        pltpu.VMEM((slots, wg.shape[1]), f32),
        pltpu.VMEM((slots, wg.shape[1]), f32),
        pltpu.VMEM((slots, wg.shape[1]), bf16),
        pltpu.VMEM((ring, cw, wg.shape[1]), bf16),
        pltpu.VMEM((ring, cw, wg.shape[1]), bf16),
        pltpu.VMEM((down_ring, wd.shape[0], cw), bf16),
        dma(kv_here + 5),
        dma(2, ring),
        dma(down_ring),
        dma(everyone),
        dma(everyone),
        dma(kv_here, 2, ranks),
        dma(kv_here, 2, ranks),
        dma(ranks),
        dma(ranks),
        dma(ranks),
        dma(ranks),
        dma(ranks),
        dma(ranks),
        dma(everyone),
        dma(everyone),
        dma(ranks),
        dma(ranks),
        dma(ranks),
        dma(ranks),
        dma(kv_here, everyone),
        dma(kv_here, everyone),
        dma(kv_here, 2, groups),
        dma(kv_here, 2, groups),
        dma(kv_here, 2),
        dma(chunks),
        dma(chunks),
        dma(chunks, ranks),
        dma(chunks, ranks),
        dma(chunks),
        dma(chunks),
        dma(chunks, ranks),
        dma(chunks, ranks),
        dma(chunks, ranks),
        dma(chunks, ranks),
        dma(chunks, ranks),
        dma(chunks, ranks),
    ]
    vmem = pl.BlockSpec(memory_space=pltpu.VMEM)
    hbm = pl.BlockSpec(memory_space=pl.ANY)
    return pl.pallas_call(
        functools.partial(step_kernel, dims),
        out_shape=(
            jax.ShapeDtypeStruct((block, model), bf16),
            jax.ShapeDtypeStruct((pages,) + pool.shape[1:], bf16),
            jax.ShapeDtypeStruct((8, 128), jnp.int32),
        ),
        in_specs=[vmem] * 6 + [hbm, vmem] + [hbm] * 5 + [vmem] + [hbm] * 3,
        out_specs=(vmem, hbm, vmem),
        scratch_shapes=scratch,
        compiler_params=pltpu.CompilerParams(
            collective_id=1, has_side_effects=True, vmem_limit_bytes=67043328
        ),
        name="fused_step",
    )(*args)


def settle_kernel(facts, arrived, mixed, pages_out, mixed_out, pages_v, mixed_v, in_sem, out_sem):
    count = pages_v.shape[0]
    copy_in = pltpu.make_async_copy(mixed, mixed_v, in_sem.at[count])
    copy_in.start()
    reads = []
    for c in range(count):
        read = pltpu.make_async_copy(arrived.at[facts[4, c]], pages_v.at[c], in_sem.at[c])
        read.start()
        reads.append(read)
    copy_in.wait()
    writes = [pltpu.make_async_copy(mixed_v, mixed_out, out_sem.at[count])]
    writes[0].start()
    for c in range(count):
        reads[c].wait()
        write = pltpu.make_async_copy(pages_v.at[c], pages_out.at[c], out_sem.at[c])
        write.start()
        writes.append(write)
    for write in writes:
        write.wait()


def settle(facts, arrived, mixed):
    hbm = pl.BlockSpec(memory_space=pl.ANY)
    count = arrived.shape[0]
    return pl.pallas_call(
        settle_kernel,
        out_shape=(
            jax.ShapeDtypeStruct(arrived.shape, arrived.dtype),
            jax.ShapeDtypeStruct(mixed.shape, mixed.dtype),
        ),
        in_specs=[pl.BlockSpec(memory_space=pltpu.SMEM), hbm, hbm],
        out_specs=(hbm, hbm),
        scratch_shapes=[
            pltpu.VMEM(arrived.shape, arrived.dtype),
            pltpu.VMEM(mixed.shape, mixed.dtype),
            pltpu.SemaphoreType.DMA((count + 1,)),
            pltpu.SemaphoreType.DMA((count + 1,)),
        ],
        name="settle",
    )(facts, arrived, mixed)


def per_device(
    hidden_states,
    attn_gain,
    mlp_gain,
    w_query,
    w_out,
    w_gate,
    w_up,
    w_down,
    kv_pool,
    resident_cache,
    resident_slot,
    resident_len,
    new_owner,
    new_local,
    new_slot,
    new_len,
    token_kv,
):
    groups = lax.axis_size("grp")
    ranks = lax.axis_size("kv")
    heads_here = w_query.shape[1] // HEAD_DIM
    kv_here = token_kv.shape[2] // HEAD_DIM
    dims = {
        "groups": groups,
        "ranks": ranks,
        "cap": groups * NPR // ranks,
        "kv_here": kv_here,
        "heads": heads_here,
    }
    mixed, arrived, facts = fused_step(
        dims,
        new_owner,
        new_local,
        new_slot,
        new_len,
        resident_slot,
        resident_len,
        hidden_states,
        attn_gain[None],
        token_kv,
        w_query,
        kv_pool,
        resident_cache[0],
        w_out.reshape(-1, w_out.shape[2]),
        mlp_gain[None],
        w_gate,
        w_up,
        w_down,
    )
    new_pages, mixed = settle(facts, arrived, mixed)
    return (mixed, new_pages[None])


def solution(mesh):
    return jax.shard_map(
        per_device,
        mesh=mesh,
        in_specs=(
            P("grp", "kv"),
            P("kv"),
            P(),
            P("kv", "tp"),
            P("tp", "kv", None),
            P(None, ("kv", "tp")),
            P(None, ("kv", "tp")),
            P(("kv", "tp"), None),
            P(("grp", "kv"), None, None, "tp"),
            P("grp", "kv", None, None, "tp"),
            P("grp", "kv"),
            P("grp", "kv"),
            P(),
            P(),
            P("grp", "kv"),
            P("grp", "kv"),
            P("grp", None, "tp"),
        ),
        out_specs=(P(("grp", "kv", "tp"), None), P("grp", "kv", None, None, "tp")),
        check_vma=False,
    )
```

time: 145 us -> 127 us (0.88)
  local copies, waits for them, and re-layouts: 11.8 us -> 0 us
  other arithmetic: 3.89 us -> 0 us
  Pallas kernels: 128 us -> 125 us
    pallas_call x1, Pallas kernels: 128 us -> 120 us  [fused_step(): pl.pallas_call(functools.partial(step_kernel, dims), out_shape=(jax.Shape...]
    gather x1 -> x0, local copies, waits for them, and re-layouts: 5.17 us -> none  [per_device(): new_pages = jnp.take(arrived, arrived_at, axis=0, mode='clip')]
    pallas_call x0 -> x1, Pallas kernels: none -> 4.81 us  [settle(): pl.pallas_call(settle_kernel, out_shape=(jax.ShapeDtypeStruct(arrived.sha...]
    reshape x7 -> x0, local copies, waits for them, and re-layouts: 3.06 us -> none  [the longest x2 0.77 us: route_tables(): new_local.reshape(groups, ranks, per_dev).transpose(1, 0, 2)]
    reduce_sum x6 -> x0, other arithmetic: 1.95 us -> none  [the longest x1 0.79 us: per_device(): slot_by = jnp.sum(jnp.where(hit, new_slot, 0), axis=1)]
    slice x1 -> x0, local copies, waits for them, and re-layouts: 1.48 us -> none  [per_device(): token_kv[:, 1]]
where the time goes in v3:
time: 127 us; the launch traced here: 126 us
  Pallas kernels  125 us (98%)
    pallas_call x1, Pallas kernels, fused_step(): pl.pallas_call(functools.partial(step_kernel, dims), out_shape=(jax.Shape...  120 us
    pallas_call x1, Pallas kernels, settle(): pl.pallas_call(settle_kernel, out_shape=(jax.ShapeDtypeStruct(arrived.sha...  4.81 us

profile of v3, /device:TPU:0, one launch (start us, length us, event | category | flops | bytes accessed | tf_op | source)
XLA Modules:
  0.0 126.0 jit_solution(882527960214594604)
XLA Ops:
  0.6 120.4 %fused_step.1 = (bf16[16,4096]{1,0:T(8,128)(2,1)}, bf16[16,2,128,512]{3,2,1,0:T(8,128)(2,1)}, s32[8,128]{1,0:T(8,128)}) custom-call(s32[4,64]{1,0:T(4,128)} %owner.1, s32[4,64]{1,0:T(4,128)} %local.1, s32[1,16]{1,0:T(1,128)} %new_slot.1, s32[1,16]{1,0:T(1,128)} %new_len.1, s32[1,8]{1,0:T(1,128)} %kept_slot.1, s32[1,8]{1,0:T(1,128)} %kept_len.1, ...), custom_call_target="tpu_custom_call" | custom-call | tf_op jit(solution)/shard_map/fused_step/pallas_call | solution.py:1117
  121.0 4.8 %settle.1 = (bf16[16,2,128,512]{3,2,1,0:T(8,128)(2,1)}, bf16[16,4096]{1,0:T(8,128)(2,1)}) custom-call(s32[8,128]{1,0:T(8,128)} %get-tuple-element.7.facts, bf16[16,2,128,512]{3,2,1,0:T(8,128)(2,1)} %get-tuple-element.8.arrived, bf16[16,4096]{1,0:T(8,128)(2,1)} %get-tuple-element.9.mixed), custom_call_target="tpu_custom_call" | custom-call | tf_op jit(solution)/shard_map/settle/pallas_call | solution.py:1158

commit v4 on v3

--- a/solution.py
+++ b/solution.py
@@ -361,7 +361,13 @@
 
     loaded = set()
 
-    def send_pages(c, kind):
+    half_page = recv_v[0].shape[1]
+    parts = [(0, 0, 0), (0, 0, half_page)]
+    parts += [(c, kind, 0) for c in range(kv_here) for kind in range(2) if c + kind]
+
+    def send_pages(n):
+        c, kind, first = parts[n]
+        tokens = pl.ds(first, recv_v[n].shape[1])
         if c not in loaded:
             loads[c].wait()
             loaded.add(c)
@@ -369,34 +375,36 @@
         def pick(i, carry):
             for a in range(cap):
                 target = lax.rem(kv + i, ranks) * cap + a
-                send_v[c][kind, i * cap + a] = pool_v[c][table[target], kind]
+                send_v[c][kind, i * cap + a, tokens] = pool_v[c][table[target], kind, tokens]
             return carry
 
         for a in range(cap):
-            recv_v[2 * c + kind][kv * cap + a] = pool_v[c][table[kv * cap + a], kind]
+            recv_v[n][kv * cap + a] = pool_v[c][table[kv * cap + a], kind, tokens]
         lax.fori_loop(1, ranks, pick, 0)
         for step in range(1, ranks):
             remote(
-                send_v[c].at[kind, pl.ds(step * cap, cap)],
-                recv_v[2 * c + kind].at[pl.ds(kv * cap, cap)],
-                page_ss.at[c, kind, step],
-                page_rs.at[c, kind, step],
+                send_v[c].at[kind, pl.ds(step * cap, cap), tokens],
+                recv_v[n].at[pl.ds(kv * cap, cap)],
+                page_ss.at[n, step],
+                page_rs.at[n, step],
                 {"kv": kv_peer(step)},
             )
 
-    def sort_pages(c, kind):
+    def sort_pages(n):
+        c, kind, first = parts[n]
+        tokens = pl.ds(first, recv_v[n].shape[1])
         for step in range(1, ranks):
             source = kv_from(step)
             arrive(
-                send_v[c].at[kind, pl.ds(step * cap, cap)],
-                recv_v[2 * c + kind].at[pl.ds(source * cap, cap)],
-                page_ss.at[c, kind, step],
-                page_rs.at[c, kind, step],
+                send_v[c].at[kind, pl.ds(step * cap, cap), tokens],
+                recv_v[n].at[pl.ds(source * cap, cap)],
+                page_ss.at[n, step],
+                page_rs.at[n, step],
                 {"kv": source},
             )
 
         def sort(i, carry):
-            sorted_v[c][kind, i] = recv_v[2 * c + kind][table[ranks * cap + i]]
+            sorted_v[c][kind, i, tokens] = recv_v[n][table[ranks * cap + i]]
             return carry
 
         lax.fori_loop(0, groups * NPR, sort, 0)
@@ -414,29 +422,32 @@
 
     every_step = tuple(range(1, groups))
 
-    def forward_pages(c, kind, steps=every_step, own=True):
+    def forward_pages(n, steps=every_step, own=True):
+        c, kind, first = parts[n]
+        tokens = pl.ds(first, recv_v[n].shape[1])
         cols = pl.ds(c * HEAD_DIM, HEAD_DIM)
         for step in steps:
             peer = grp_peer(step)
             remote(
-                sorted_v[c].at[kind, pages_of(peer)],
-                arrived_out.at[pages_of(grp), kind, :, cols],
-                z_ss.at[c, kind, step],
-                z_rs.at[c, kind, step],
+                sorted_v[c].at[kind, pages_of(peer), tokens],
+                arrived_out.at[pages_of(grp), kind, tokens, cols],
+                z_ss.at[n, step],
+                z_rs.at[n, step],
                 {"grp": peer},
             )
         if not own:
             return
         store = pltpu.make_async_copy(
-            sorted_v[c].at[kind, pages_of(grp)],
-            arrived_out.at[pages_of(grp), kind, :, cols],
-            z_own.at[c, kind],
+            sorted_v[c].at[kind, pages_of(grp), tokens],
+            arrived_out.at[pages_of(grp), kind, tokens, cols],
+            z_own.at[n],
         )
         store.start()
         stores.append(store)
 
-    send_pages(0, 0)
-    send_pages(0, 1)
+    send_pages(0)
+    send_pages(1)
+    send_pages(2)
 
     load_h.wait()
     load_q.wait()
@@ -522,12 +533,14 @@
             near_q_send.at[peer], near_q_recv.at[kv], nq_ss.at[step], nq_rs.at[step], {"kv": peer}
         )
         remote(own_send, own_recv.at[kv], own_ss.at[step], own_rs.at[step], {"kv": peer})
-    send_pages(1, 0)
-    send_pages(1, 1)
-    sort_pages(0, 0)
-    forward_pages(0, 0)
-    sort_pages(0, 1)
-    forward_pages(0, 1)
+    send_pages(3)
+    send_pages(4)
+    sort_pages(0)
+    forward_pages(0)
+    sort_pages(1)
+    forward_pages(1)
+    sort_pages(2)
+    forward_pages(2)
 
     for step in range(1, ranks):
         source = kv_from(step)
@@ -562,9 +575,9 @@
             far_q_send.at[peer], far_q_recv.at[me], fq_ss.at[step], fq_rs.at[step], flat(peer)
         )
 
-    send_pages(2, 0)
-    sort_pages(1, 0)
-    forward_pages(1, 0)
+    send_pages(5)
+    sort_pages(3)
+    forward_pages(3)
 
     row_id = rows_of((8, 128))
     row_masks = [
@@ -655,10 +668,12 @@
     for step in range(1, ranks):
         peer = kv_peer(step)
         remote(near_send.at[peer], near_recv.at[kv], na_ss.at[step], na_rs.at[step], {"kv": peer})
-    send_pages(2, 1)
-    send_pages(3, 0)
-    send_pages(3, 1)
-
+    send_pages(6)
+    send_pages(7)
+    send_pages(8)
+
+    sort_pages(4)
+    forward_pages(4)
     for step in range(1, everyone):
         source = all_from(step)
         arrive(
@@ -770,14 +785,12 @@
         return (gathered + own_weight * own_piece) / total
 
     far_attention(0)
-    sort_pages(1, 1)
     far_attention(1)
-    forward_pages(1, 1)
-    sort_pages(2, 0)
-    sort_pages(2, 1)
+    sort_pages(5)
+    middle = groups // 2
+    forward_pages(5, (middle,), False)
+    sort_pages(6)
     far_attention(2)
-    middle = groups // 2
-    forward_pages(2, 0, (middle,), False)
     onehot_t[...] = jnp.transpose(onehot[...]).astype(jnp.bfloat16)
     for at in range(used, all_lse.shape[0], 8):
         all_lse[at : at + 8, :] = jnp.zeros((8, 128), jnp.float32)
@@ -804,13 +817,13 @@
         mine = hidden[:, i * cw : (i + 1) * cw].reshape(ranks, 2, rows16, cw)
         mine = jnp.where(tp == 0, mine[:, 0], mine[:, 1]).reshape(half, cw)
         feature_v[i] = mine.astype(jnp.float32)
-    sort_pages(3, 0)
-    sort_pages(3, 1)
+    sort_pages(7)
+    sort_pages(8)
     far_attention(3)
-    forward_pages(2, 0, tuple(step for step in every_step if step != middle))
-    forward_pages(2, 1)
-    forward_pages(3, 0)
-    forward_pages(3, 1)
+    forward_pages(5, tuple(step for step in every_step if step != middle))
+    forward_pages(6)
+    forward_pages(7)
+    forward_pages(8)
     fits = 128 // chunk_lanes
     for c in range(kv_here):
         wait_far(c)
@@ -975,18 +988,18 @@
         total = scatter_end(c, (d2_send, d2_recv), (d2_ss, d2_rs))
         total = total + kept_v[c].astype(jnp.float32)
         mixed_out[:, c * cw : (c + 1) * cw] = total.astype(jnp.bfloat16)
-    for c in range(kv_here):
+    for n, (c, kind, first) in enumerate(parts):
+        tokens = pl.ds(first, recv_v[n].shape[1])
         cols = pl.ds(c * HEAD_DIM, HEAD_DIM)
-        for kind in range(2):
-            for step in range(1, groups):
-                source = grp_from(step)
-                arrive(
-                    sorted_v[c].at[kind, pages_of(source)],
-                    arrived_out.at[pages_of(source), kind, :, cols],
-                    z_ss.at[c, kind, step],
-                    z_rs.at[c, kind, step],
-                    {"grp": source},
-                )
+        for step in range(1, groups):
+            source = grp_from(step)
+            arrive(
+                sorted_v[c].at[kind, pages_of(source), tokens],
+                arrived_out.at[pages_of(source), kind, tokens, cols],
+                z_ss.at[n, step],
+                z_rs.at[n, step],
+                {"grp": source},
+            )
     for store in stores:
         store.wait()
     for copy in pending:
@@ -1018,7 +1031,7 @@
     f32, bf16 = jnp.float32, jnp.bfloat16
     whole = lambda count: pltpu.VMEM((count, 2, tokens, HEAD_DIM), bf16)
     pair = lambda count: pltpu.VMEM((2, count, tokens, HEAD_DIM), bf16)
-    single = lambda count: pltpu.VMEM((count, tokens, HEAD_DIM), bf16)
+    single = lambda count, length: pltpu.VMEM((count, length, HEAD_DIM), bf16)
     dma = lambda *shape: pltpu.SemaphoreType.DMA(shape)
     scratch = [
         pltpu.SMEM((2 * pages,), jnp.int32),
@@ -1029,7 +1042,7 @@
         pltpu.VMEM(token_kv.shape, bf16),
         [whole(pool.shape[0]) for _ in range(kv_here)],
         [pair(pages) for _ in range(kv_here)],
-        [single(pages) for _ in range(2 * kv_here)],
+        [single(pages, tokens // 2)] * 2 + [single(pages, tokens)] * (2 * kv_here - 1),
         [pair(pages) for _ in range(kv_here)],
         pltpu.VMEM(res.shape, bf16),
         pltpu.VMEM(wq.shape, bf16),
@@ -1080,8 +1093,8 @@
         dma(down_ring),
         dma(everyone),
         dma(everyone),
-        dma(kv_here, 2, ranks),
-        dma(kv_here, 2, ranks),
+        dma(2 * kv_here + 1, ranks),
+        dma(2 * kv_here + 1, ranks),
         dma(ranks),
         dma(ranks),
         dma(ranks),
@@ -1096,9 +1109,9 @@
         dma(ranks),
         dma(kv_here, everyone),
         dma(kv_here, everyone),
-        dma(kv_here, 2, groups),
-        dma(kv_here, 2, groups),
-        dma(kv_here, 2),
+        dma(2 * kv_here + 1, groups),
+        dma(2 * kv_here + 1, groups),
+        dma(2 * kv_here + 1),
         dma(chunks),
         dma(chunks),
         dma(chunks, ranks),

time: 127 us -> 124 us (0.976)
  Pallas kernels: 125 us -> 122 us
    pallas_call x1, Pallas kernels: 120 us -> 117 us  [fused_step(): pl.pallas_call(functools.partial(step_kernel, dims), out_shape=(jax.Shape...]
where the time goes in v4:
time: 124 us; the launch traced here: 123 us
  Pallas kernels  122 us (98%)
    pallas_call x1, Pallas kernels, fused_step(): pl.pallas_call(functools.partial(step_kernel, dims), out_shape=(jax.Shape...  117 us
    pallas_call x1, Pallas kernels, settle(): pl.pallas_call(settle_kernel, out_shape=(jax.ShapeDtypeStruct(arrived.sha...  4.81 us

profile of v4, /device:TPU:0, one launch (start us, length us, event | category | flops | bytes accessed | tf_op | source)
XLA Modules:
  0.0 122.9 jit_solution(2192655102595998975)
XLA Ops:
  0.6 117.3 %fused_step.1 = (bf16[16,4096]{1,0:T(8,128)(2,1)}, bf16[16,2,128,512]{3,2,1,0:T(8,128)(2,1)}, s32[8,128]{1,0:T(8,128)}) custom-call(s32[4,64]{1,0:T(4,128)} %owner.1, s32[4,64]{1,0:T(4,128)} %local.1, s32[1,16]{1,0:T(1,128)} %new_slot.1, s32[1,16]{1,0:T(1,128)} %new_len.1, s32[1,8]{1,0:T(1,128)} %kept_slot.1, s32[1,8]{1,0:T(1,128)} %kept_len.1, ...), custom_call_target="tpu_custom_call" | custom-call | tf_op jit(solution)/shard_map/fused_step/pallas_call | solution.py:1130
  117.9 4.8 %settle.1 = (bf16[16,2,128,512]{3,2,1,0:T(8,128)(2,1)}, bf16[16,4096]{1,0:T(8,128)(2,1)}) custom-call(s32[8,128]{1,0:T(8,128)} %get-tuple-element.7.facts, bf16[16,2,128,512]{3,2,1,0:T(8,128)(2,1)} %get-tuple-element.8.arrived, bf16[16,4096]{1,0:T(8,128)(2,1)} %get-tuple-element.9.mixed), custom_call_target="tpu_custom_call" | custom-call | tf_op jit(solution)/shard_map/settle/pallas_call | solution.py:1171

commit v5 on v4

--- a/solution.py
+++ b/solution.py
@@ -420,7 +420,7 @@
 
     stores = []
 
-    every_step = tuple(range(1, groups))
+    every_step = tuple(sorted(range(1, groups), key=lambda step: step != groups // 2))
 
     def forward_pages(n, steps=every_step, own=True):
         c, kind, first = parts[n]

time: 124 us -> 124 us (level)
  no operation moved by 1% of the time
where the time goes in v5:
time: 124 us; the launch traced here: 123 us
  Pallas kernels  122 us (98%)
    pallas_call x1, Pallas kernels, fused_step(): pl.pallas_call(functools.partial(step_kernel, dims), out_shape=(jax.Shape...  117 us
    pallas_call x1, Pallas kernels, settle(): pl.pallas_call(settle_kernel, out_shape=(jax.ShapeDtypeStruct(arrived.sha...  4.81 us

profile of v5, /device:TPU:0, one launch (start us, length us, event | category | flops | bytes accessed | tf_op | source)
XLA Modules:
  0.0 123.0 jit_solution(17636429161228637683)
XLA Ops:
  0.6 117.4 %fused_step.1 = (bf16[16,4096]{1,0:T(8,128)(2,1)}, bf16[16,2,128,512]{3,2,1,0:T(8,128)(2,1)}, s32[8,128]{1,0:T(8,128)}) custom-call(s32[4,64]{1,0:T(4,128)} %owner.1, s32[4,64]{1,0:T(4,128)} %local.1, s32[1,16]{1,0:T(1,128)} %new_slot.1, s32[1,16]{1,0:T(1,128)} %new_len.1, s32[1,8]{1,0:T(1,128)} %kept_slot.1, s32[1,8]{1,0:T(1,128)} %kept_len.1, ...), custom_call_target="tpu_custom_call" | custom-call | tf_op jit(solution)/shard_map/fused_step/pallas_call | solution.py:1130
  118.0 4.8 %settle.1 = (bf16[16,2,128,512]{3,2,1,0:T(8,128)(2,1)}, bf16[16,4096]{1,0:T(8,128)(2,1)}) custom-call(s32[8,128]{1,0:T(8,128)} %get-tuple-element.7.facts, bf16[16,2,128,512]{3,2,1,0:T(8,128)(2,1)} %get-tuple-element.8.arrived, bf16[16,4096]{1,0:T(8,128)(2,1)} %get-tuple-element.9.mixed), custom_call_target="tpu_custom_call" | custom-call | tf_op jit(solution)/shard_map/settle/pallas_call | solution.py:1171
